TPU v7x, 64 devices: a 2x2x8 block of a 4x4x8 slice. The times are simulated.
64 devices in a mesh: data: 4 (over x, y), sp: 16 (over z, core).
Axes of the slice: x: 2, y: 2, z: 8, core: 2. Of those that a mesh axis runs over, the one named last changes fastest.
The devices are a block of a 4x4x8 slice.
Arguments:
- latents: bfloat16 [8, 32, 512, 1152], P('data', 'sp'), parts along dimension 0
- valid_len: int32 [8], P('data'), parts along dimension 0
- norm_w: bfloat16 [2, 4, 1152], replicated
- w_qkv: bfloat16 [2, 1152, 3456], replicated
- w_out: bfloat16 [2, 16, 72, 1152], replicated
- w_up: bfloat16 [2, 1152, 4608], replicated
- w_down: bfloat16 [2, 4608, 1152], replicated
Outputs:
- output: bfloat16 [8, 32, 512, 1152], P('data', 'sp'), parts along dimension 0
There are 4 independent parts. A program takes and returns all parts, laid end to end along the dimension named above; an argument that names none is the same for every part.
All inputs are finite; a program needn't handle non-finite values.
Results may differ from a plain program's by a relative error of at most 0.0158405.
Values are sent between devices in bfloat16 or wider.
A program may use at most 768 MiB of HBM per device.

v0:
```python
import jax
import jax.numpy as jnp
from jax import lax
from jax.sharding import PartitionSpec as P

LN_EPS = 1e-6
NEG_BIG = -1e30


def layer_norm(tokens, ln_gain, ln_shift):
    values = tokens.astype(jnp.float32)
    average = jnp.mean(values, axis=-1, keepdims=True)
    centered = values - average
    variance = jnp.mean(centered * centered, axis=-1, keepdims=True)
    normed = centered * lax.rsqrt(variance + LN_EPS)
    return (normed * ln_gain.astype(jnp.float32) + ln_shift.astype(jnp.float32)).astype(jnp.bfloat16)


def project(tokens, weight):
    return jnp.dot(tokens, weight, preferred_element_type=jnp.float32).astype(jnp.bfloat16)


def residual(base_act, delta_act):
    return (base_act.astype(jnp.float32) + delta_act.astype(jnp.float32)).astype(jnp.bfloat16)


def attention(qkv_proj, num_heads, seq_axis, valid_len):
    model_width = qkv_proj.shape[-1] // 3
    head_dim = model_width // num_heads
    lead_shape = qkv_proj.shape[:-1]
    split_heads = qkv_proj.reshape(lead_shape + (3, num_heads, head_dim))
    query_h = split_heads[..., 0, :, :]
    key_h = split_heads[..., 1, :, :]
    value_h = split_heads[..., 2, :, :]
    seq_len = qkv_proj.shape[seq_axis]
    tile_len = min(seq_len, 128)
    score_scale = head_dim ** -0.5
    if seq_axis == 2:
        score_form = 'btqhd,btkhd->bthqk'
        out_form = 'bthqk,btkhd->btqhd'
    else:
        score_form = 'bqshd,bkshd->bshqk'
        out_form = 'bshqk,bkshd->bqshd'
    key_pos = jnp.arange(seq_len)[None, None, None, None, :]

    def one_tile(tile_idx):
        tile_start = tile_idx * tile_len
        query_tile = lax.dynamic_slice_in_dim(query_h, tile_start, tile_len, seq_axis)
        scores = jnp.einsum(score_form, query_tile, key_h, preferred_element_type=jnp.float32) * score_scale
        if seq_axis == 1:
            query_pos = (tile_start + jnp.arange(tile_len))[None, None, None, :, None]
            allowed = (key_pos <= query_pos) & (key_pos < valid_len[:, None, None, None, None])
            scores = jnp.where(allowed, scores, NEG_BIG)
        attn_prob = jax.nn.softmax(scores, axis=-1).astype(jnp.bfloat16)
        return jnp.einsum(out_form, attn_prob, value_h, preferred_element_type=jnp.float32).astype(jnp.bfloat16)

    tile_outs = lax.map(one_tile, jnp.arange(seq_len // tile_len))
    return jnp.moveaxis(tile_outs, 0, seq_axis).reshape(lead_shape + (model_width,))


def value_a9(tokens, layer_idx, params, seq_axis, valid_len):
    norm_w, w_qkv, w_out, w_up, w_down = params
    num_heads = w_out.shape[1]
    model_width = tokens.shape[-1]
    normed = layer_norm(tokens, norm_w[layer_idx, 0], norm_w[layer_idx, 1])
    attn_out = attention(project(normed, w_qkv[layer_idx]), num_heads, seq_axis, valid_len)
    hidden = residual(tokens, project(attn_out, w_out[layer_idx].reshape(model_width, model_width)))
    normed_mlp = layer_norm(hidden, norm_w[layer_idx, 2], norm_w[layer_idx, 3])
    gelu_act = jax.nn.gelu(project(normed_mlp, w_up[layer_idx]).astype(jnp.float32), approximate=True).astype(jnp.bfloat16)
    return residual(hidden, project(gelu_act, w_down[layer_idx]))


def solution(mesh):
    act_spec = P('data', 'sp', None, None)

    def local_step(latents, valid_len, norm_w, w_qkv, w_out, w_up, w_down):
        params = (norm_w, w_qkv, w_out, w_up, w_down)
        spatial = value_a9(latents, 0, params, 2, valid_len)
        by_patch = lax.all_to_all(spatial, 'sp', 2, 1, tiled=True)
        temporal = value_a9(by_patch, 1, params, 1, valid_len)
        return lax.all_to_all(temporal, 'sp', 1, 2, tiled=True)

    return jax.shard_map(local_step, mesh=mesh, in_specs=(act_spec, P('data'), P(), P(), P(), P(), P()), out_specs=act_spec, check_vma=False)
```

profile of v0, /device:TPU:21, one launch (start us, length us, event | category | flops | bytes accessed | tf_op | source)
XLA Modules:
  0.0 771.6 jit_solution(9232394310417701370)
XLA Ops:
  8.6 25.2 %convolution_convert_fusion.1 = bf16[2,2,512,3456]{3,2,1,0:T(8,128)(2,1)} fusion(bf16[2,1152,3456]{2,1,0:T(8,128)(2,1)} %param.12, bf16[2,2,512,1152]{3,2,1,0:T(8,128)(2,1)S(1)} %bitcast.158, f32[1152]{0:T(1024)S(1)} %get-tuple-element.64, f32[1152]{0:T(1024)S(1)} %get-tuple-element.65, f32[2,2,512]{2,1,0:T(2,128)S(1)} %add_rsqrt_fusion.3, ...), kind=kOutput, calls=%fused_computation.60 | convolution fusion | flops 16328687616 | bytes 26862592 | tf_op jit(solution)/shard_map/dot_general | solution.py:20
  33.9 18.7 %copy.29 = bf16[2,2,512,3456]{2,3,1,0:T(8,128)(2,1)} copy(bf16[2,2,512,3456]{3,2,1,0:T(8,128)(2,1)} %convolution_convert_fusion.1) | data formatting | bytes 28311552 | tf_op jit(solution)/shard_map/convert_element_type | solution.py:20
  52.5 11.1 %slice_bitcast_fusion = (bf16[2,2,512,16,72]{2,4,3,1,0:T(8,128)(2,1)}, bf16[2,2,512,16,72]{2,4,3,1,0:T(8,128)(2,1)}, bf16[2,2,512,16,72]{2,4,3,1,0:T(8,128)(2,1)}) fusion(bf16[2,2,512,3,16,72]{2,5,4,3,1,0:T(8,128)(2,1)} %bitcast.156), kind=kLoop, calls=%fused_computation.109 | loop fusion | bytes 28311552 | tf_op jit(solution)/shard_map/squeeze | solution.py:34
  63.6 88.5 %while.2 = (s32[]{:T(128)}, bf16[4,2,2,128,16,72]{3,5,4,2,1,0:T(8,128)(2,1)}, s32[4]{0:T(128)S(1)}, bf16[2,2,512,16,72]{2,4,3,1,0:T(8,128)(2,1)}, bf16[2,2,512,1...) while((s32[]{:T(128)}, ...), condition=%wide.region_5.6_spmd, body=%wide.region_2.5_spmd.sunk | while | flops 1229521408 | bytes 45417120 | solution.py:57
  65.0 10.9 %fusion.210 = (f32[2,2,16,128]{3,2,1,0:T(8,128)S(1)}, f32[2,2,16,128,512]{4,3,2,1,0:T(8,128)}) fusion(bf16[2,2,512,16,72]{2,4,3,1,0:T(8,128)(2,1)} %get-tuple-element.160, bf16[2,2,512,16,72]{2,4,3,1,0:T(8,128)(2,1)} %get-tuple-element.159, s32[]{:T(128)S(6)} %select_n.22), kind=kOutput, calls=%fused_computation.153.clone.1 | convolution fusion | flops 616563200 | bytes 22708228 | tf_op jit(solution)/shard_map/while/body/eval_jaxpr/sub | solution.py:54
  87.1 10.9 %fusion.210 = (f32[2,2,16,128]{3,2,1,0:T(8,128)S(1)}, f32[2,2,16,128,512]{4,3,2,1,0:T(8,128)}) fusion(bf16[2,2,512,16,72]{2,4,3,1,0:T(8,128)(2,1)} %get-tuple-element.160, bf16[2,2,512,16,72]{2,4,3,1,0:T(8,128)(2,1)} %get-tuple-element.159, s32[]{:T(128)S(6)} %select_n.22), kind=kOutput, calls=%fused_computation.153.clone.1 | convolution fusion | flops 616563200 | bytes 22708228 | tf_op jit(solution)/shard_map/while/body/eval_jaxpr/sub | solution.py:54
  109.2 10.9 %fusion.210 = (f32[2,2,16,128]{3,2,1,0:T(8,128)S(1)}, f32[2,2,16,128,512]{4,3,2,1,0:T(8,128)}) fusion(bf16[2,2,512,16,72]{2,4,3,1,0:T(8,128)(2,1)} %get-tuple-element.160, bf16[2,2,512,16,72]{2,4,3,1,0:T(8,128)(2,1)} %get-tuple-element.159, s32[]{:T(128)S(6)} %select_n.22), kind=kOutput, calls=%fused_computation.153.clone.1 | convolution fusion | flops 616563200 | bytes 22708228 | tf_op jit(solution)/shard_map/while/body/eval_jaxpr/sub | solution.py:54
  131.3 10.9 %fusion.210 = (f32[2,2,16,128]{3,2,1,0:T(8,128)S(1)}, f32[2,2,16,128,512]{4,3,2,1,0:T(8,128)}) fusion(bf16[2,2,512,16,72]{2,4,3,1,0:T(8,128)(2,1)} %get-tuple-element.160, bf16[2,2,512,16,72]{2,4,3,1,0:T(8,128)(2,1)} %get-tuple-element.159, s32[]{:T(128)S(6)} %select_n.22), kind=kOutput, calls=%fused_computation.153.clone.1 | convolution fusion | flops 616563200 | bytes 22708228 | tf_op jit(solution)/shard_map/while/body/eval_jaxpr/sub | solution.py:54
  152.2 10.5 %copy.30 = bf16[2,2,4,128,16,72]{3,2,5,4,1,0:T(4,128)(2,1)} copy(bf16[2,2,4,128,16,72]{3,5,4,1,0,2:T(8,128)(2,1)} %bitcast.165) | data formatting | bytes 9437184 | tf_op jit(solution)/shard_map/transpose | solution.py:58
  189.0 38.8 %fusion.196 = bf16[2,2,512,4608]{3,2,1,0:T(8,128)(2,1)} fusion(bf16[2,1152,4608]{2,1,0:T(8,128)(2,1)} %param.14, bf16[2,2,512,1152]{3,2,1,0:T(8,128)(2,1)} %copy-done.1, f32[1152]{0:T(1024)S(1)} %copy-done.8, f32[1152]{0:T(1024)S(1)} %copy-done.9, f32[2,2,512]{2,1,0:T(2,128)S(1)} %add_rsqrt_fusion.2, ...), kind=kOutput, calls=%fused_computation.31.clone.clone.clone.clone.clone.clone.2 | convolution fusion | flops 21861236736 | bytes 34235392 | tf_op jit(solution)/shard_map/dot_general | solution.py:20
  227.8 32.1 %fusion.73 = bf16[2,2,512,1152]{3,2,1,0:T(8,128)(2,1)} fusion(bf16[2,2,512,1152]{3,2,1,0:T(8,128)(2,1)} %copy-done.1, bf16[2,4608,1152]{2,1,0:T(8,128)(2,1)} %param.15, bf16[2,2,512,4608]{3,2,1,0:T(8,128)(2,1)} %fusion.196), kind=kOutput, calls=%fused_computation.84 | convolution fusion | flops 21755068416 | bytes 38928384 | tf_op jit(solution)/shard_map/dot_general | solution.py:20
  269.2 11.3 %all-to-all-start = ((bf16[2,2,512,1152]{3,1,0,2:T(2,128)(2,1)}), bf16[2,2,512,1152]{3,1,0,2:T(2,128)(2,1)}, u32[]{:S(2)}, u32[]{:S(2)}) async-start(bf16[2,2,512,1152]{3,1,0,2:T(2,128)(2,1)} %copy.32), calls=%async_computation | async-start | bytes 9437184 | tf_op jit(solution)/shard_map/all_to_all | solution.py:79
  280.7 104.8 %all-to-all-done = bf16[2,2,512,1152]{3,1,0,2:T(2,128)(2,1)} async-done(((bf16[2,2,512,1152]{3,1,0,2:T(2,128)(2,1)}), bf16[2,2,512,1152]{3,1,0,2:T(2,128)(2,1)}, u32[]{:S(2)}, u32[]{:S(2)}) %all-to-all-start) | async-done | bytes 4718624 | tf_op jit(solution)/shard_map/all_to_all | solution.py:79
  394.6 24.6 %convolution_convert_fusion = bf16[2,32,32,3456]{3,2,1,0:T(8,128)(2,1)} fusion(bf16[2,32,32,1152]{3,2,1,0:T(8,128)(2,1)S(1)} %bitcast.166, bf16[2,1152,3456]{2,1,0:T(8,128)(2,1)} %param.12), kind=kOutput, calls=%fused_computation.59 | convolution fusion | flops 16314531840 | bytes 26836992 | tf_op jit(solution)/shard_map/dot_general | solution.py:20
  419.2 49.4 %reshape.189 = bf16[2,32,32,3,16,72]{5,4,3,2,1,0:T(8,128)(2,1)} reshape(bf16[2,32,32,3456]{3,2,1,0:T(8,128)(2,1)} %convolution_convert_fusion) | data formatting | bytes 28311552 | tf_op jit(solution)/shard_map/reshape | solution.py:31
  468.6 17.0 %fusion.159 = (bf16[2,32,32,1,16,72]{5,4,3,2,1,0:T(8,128)(2,1)}, bf16[2,32,32,1,16,72]{5,4,3,2,1,0:T(8,128)(2,1)}, bf16[2,32,32,1,16,72]{5,4,3,2,1,0:T(8,128)(2,1)}) fusion(bf16[2,32,32,3,16,72]{5,4,3,2,1,0:T(8,128)(2,1)} %reshape.189), kind=kLoop, calls=%fused_computation.154 | loop fusion | bytes 28311552 | tf_op jit(solution)/shard_map/slice | solution.py:34
  485.7 22.6 %fusion.76 = f32[2,32,16,32,32]{3,4,2,1,0:T(8,128)} fusion(bf16[2,32,32,1,16,72]{5,4,3,2,1,0:T(8,128)(2,1)} %get-tuple-element.83, bf16[2,32,32,1,16,72]{5,4,3,2,1,0:T(8,128)(2,1)} %get-tuple-element.82), kind=kOutput, calls=%fused_computation.93 | convolution fusion | flops 150994944 | bytes 13631488 | tf_op jit(solution)/shard_map/while/body/eval_jaxpr/bqshd,bkshd->bshqk/dot_general | solution.py:49
  508.3 20.6 %fusion.161 = (f32[2,32,16,32]{3,2,1,0:T(8,128)S(1)}, f32[2,32,16,32,32]{3,4,2,1,0:T(8,128)}) fusion(f32[2,32,16,32,32]{3,4,2,1,0:T(8,128)} %fusion.76, pred[2,32,32]{1,2,0:T(8,128)(4,1)S(1)} %broadcast_and_fusion), kind=kOutput, calls=%fused_computation.156 | output fusion | flops 6291487 | bytes 8521728 | tf_op jit(solution)/shard_map/while/body/eval_jaxpr/sub | solution.py:54
  528.9 14.2 %convert_bitcast_fusion = bf16[2,32,32,16,72]{4,1,3,2,0:T(8,128)(2,1)} fusion(f32[2,32,16,32,32]{3,4,2,1,0:T(8,128)} %get-tuple-element.92, f32[2,32,16,32]{3,2,1,0:T(8,128)S(1)} %get-tuple-element.91, bf16[2,32,32,1,16,72]{5,4,3,2,1,0:T(8,128)(2,1)} %get-tuple-element.81), kind=kOutput, calls=%fused_computation.96 | convolution fusion | flops 155451392 | bytes 13762560 | tf_op jit(solution)/shard_map/while/body/eval_jaxpr/bshqk,bkshd->bqshd/dot_general | solution.py:55
  543.1 9.8 %copy.38 = bf16[2,32,32,16,72]{4,3,2,1,0:T(8,128)(2,1)} copy(bf16[2,32,32,16,72]{4,1,3,2,0:T(8,128)(2,1)} %convert_bitcast_fusion) | data formatting | bytes 9437184 | tf_op jit(solution)/shard_map/while/body/eval_jaxpr/convert_element_type | solution.py:55
  552.9 14.0 %reshape_transpose.3 = bf16[2,32,32,1152]{3,2,1,0:T(8,128)(2,1)} reshape(bf16[2,32,32,16,72]{4,3,2,1,0:T(8,128)(2,1)} %copy.38) | data formatting | bytes 9437184 | tf_op jit(solution)/shard_map/reshape;transpose | solution.py:58
  582.4 38.7 %fusion.200 = bf16[2,32,32,4608]{3,2,1,0:T(8,128)(2,1)} fusion(bf16[2,1152,4608]{2,1,0:T(8,128)(2,1)} %param.14, bf16[2,32,32,1152]{3,2,1,0:T(8,128)(2,1)} %copy-done, f32[1152]{0:T(1024)S(1)} %copy-done.7, f32[1152]{0:T(1024)S(1)} %copy-done.6, f32[2,32,32]{2,1,0:T(8,128)S(1)} %add_rsqrt_fusion, ...), kind=kOutput, calls=%fused_computation.37.clone.clone.clone.clone.clone.clone.2 | convolution fusion | flops 21861236736 | bytes 34235392 | tf_op jit(solution)/shard_map/dot_general | solution.py:20
  621.1 30.9 %fusion.74 = bf16[2,32,32,1152]{3,2,1,0:T(8,128)(2,1)S(1)} fusion(bf16[2,32,32,1152]{3,2,1,0:T(8,128)(2,1)} %copy-done, bf16[2,4608,1152]{2,1,0:T(8,128)(2,1)} %param.15, bf16[2,32,32,4608]{3,2,1,0:T(8,128)(2,1)} %fusion.200), kind=kOutput, calls=%fused_computation.85 | convolution fusion | flops 21755068416 | bytes 38928384 | tf_op jit(solution)/shard_map/dot_general | solution.py:20
  652.7 115.9 %all_to_all.27 = bf16[2,32,32,1152]{3,2,0,1:T(8,128)(2,1)S(1)} all-to-all(bf16[2,32,32,1152]{3,2,0,1:T(8,128)(2,1)S(1)} %copy.39), channel_id=1, replica_groups=mesh['data'=4,'sp'=16] {'sp'}, dimensions={1} | all-to-all | bytes 9437184 | tf_op jit(solution)/shard_map/all_to_all | solution.py:81
  (75 shorter events, 113.8 us)
Async XLA Ops:
  0.0 8.6 %slice-start = ((s8[4718592]{0:T(1024)(128)(4,1)}), s8[524288]{0:T(1024)(128)(4,1)S(1)}, s32[]{:S(2)}) async-start(s8[4718592]{0:T(1024)(128)(4,1)} %bitcast.157), calls=%async_computation.2 | async-start | bytes 1048576
  1.6 7.0 slice-start.1
  162.7 12.7 %slice-start.2 = ((s8[4718592]{0:T(1024)(128)(4,1)}), s8[524288]{0:T(1024)(128)(4,1)S(1)}, s32[]{:S(2)}) async-start(s8[4718592]{0:T(1024)(128)(4,1)} %bitcast.159), calls=%async_computation.4 | async-start | bytes 1048576
  170.8 4.6 slice-start.3
  170.8 6.2 copy-start.2
  177.0 12.0 %copy-start.8 = (f32[1152]{0:T(1024)S(1)}, f32[1152]{0:T(1024)}, u32[]{:S(2)}) copy-start(f32[1152]{0:T(1024)} %get-tuple-element.62) | copy-start | bytes 13828
  177.0 12.0 %copy-start.9 = (f32[1152]{0:T(1024)S(1)}, f32[1152]{0:T(1024)}, u32[]{:S(2)}) copy-start(f32[1152]{0:T(1024)} %get-tuple-element.63) | copy-start | bytes 13828
  185.3 2.2 copy-start.1
  259.9 20.6 %copy-start.10 = (s32[2]{0:T(128)S(1)}, s32[2]{0:T(128)}, u32[]{:S(2)}) copy-start(s32[2]{0:T(128)} %param.10) | copy-start | bytes 28
  269.2 116.3 %all-to-all-start = ((bf16[2,2,512,1152]{3,1,0,2:T(2,128)(2,1)}), bf16[2,2,512,1152]{3,1,0,2:T(2,128)(2,1)}, u32[]{:S(2)}, u32[]{:S(2)}) async-start(bf16[2,2,512,1152]{3,1,0,2:T(2,128)(2,1)} %copy.32), calls=%async_computation | async-start | bytes 9437184 | tf_op jit(solution)/shard_map/all_to_all | solution.py:79
  391.0 1.9 copy-start.4
  391.0 1.9 copy-start.5
  567.0 3.8 slice-start.4
  567.0 4.4 copy-start.3
  567.0 4.5 slice-start.5
  571.4 10.9 %copy-start.6 = (f32[1152]{0:T(1024)S(1)}, f32[1152]{0:T(1024)}, u32[]{:S(2)}) copy-start(f32[1152]{0:T(1024)} %get-tuple-element.59) | copy-start | bytes 13828
  571.4 10.9 %copy-start.7 = (f32[1152]{0:T(1024)S(1)}, f32[1152]{0:T(1024)}, u32[]{:S(2)}) copy-start(f32[1152]{0:T(1024)} %get-tuple-element.66) | copy-start | bytes 13828
  578.7 2.2 copy-start
where the time goes:
time: 781 us; the launch traced here: 772 us
  matrix products  326 us (42%)
  local copies, waits for them, and re-layouts  169 us (22%)
  blocking collectives  116 us (15%)
  waiting for transfers between devices  105 us (13%)
  other arithmetic  41.2 us (5%)
  starting transfers between devices  11.3 us (1%)
    dot_general x8, matrix products, project(): jnp.dot(tokens, weight, preferred_element_type=jnp.float32)  206 us
    all_to_all x1, blocking collectives, local_step(): return lax.all_to_all(temporal, 'sp', 1, 2, tiled=True)  116 us
    all_to_all x1, waiting for transfers between devices, local_step(): by_patch = lax.all_to_all(spatial, 'sp', 2, 1, tiled=True)  105 us
    dot_general x5, matrix products, one_tile(): jnp.einsum(out_form, attn_prob, value_h, preferred_element_type=jnp.float32)  53.4 us
    reshape x1, local copies, waits for them, and re-layouts, attention(): split_heads = qkv_proj.reshape(lead_shape + (3, num_heads, head_dim))  49.4 us
    sub x4, matrix products, one_tile(): attn_prob = jax.nn.softmax(scores, axis=-1).astype(jnp.bfloat16)  43.7 us
    dot_general x1, matrix products, one_tile(): jnp.einsum(score_form, query_tile, key_h, preferred_element_type=jnp.floa...  22.6 us
    sub x1, other arithmetic, one_tile(): attn_prob = jax.nn.softmax(scores, axis=-1).astype(jnp.bfloat16)  20.6 us
  transfers between devices with their start and end apart: 1, of which 1 were waited for; matrix products, arithmetic and copies ran while one was open for 0% of the time, Pallas kernels for 0%

commit v1 on v0

v1 whole, which is shorter than its diff:
```python
import functools
import math

import jax
import jax.numpy as jnp
from jax import lax
from jax.experimental import pallas as pl
from jax.experimental.pallas import tpu as pltpu
from jax.sharding import PartitionSpec as P

LN_EPS = 1e-6
MASKED = -1e30
OPEN = 3e38
LANES = 128
f32, bf16 = jnp.float32, jnp.bfloat16
MESH = pl.DeviceIdType.MESH


def layer_norm(tokens, gain, shift):
    values = tokens.astype(f32)
    inv_width = 1.0 / values.shape[-1]
    centered = values - jnp.sum(values, -1, keepdims=True) * inv_width
    variance = jnp.sum(centered * centered, -1, keepdims=True) * inv_width
    return (centered * lax.rsqrt(variance + LN_EPS) * gain + shift).astype(bf16)


def project(a, b):
    return jnp.dot(a, b, preferred_element_type=f32).astype(bf16)


def residual(base, delta):
    return (base.astype(f32) + delta.astype(f32)).astype(bf16)


def gelu(u):
    x = u.astype(f32)
    c = math.sqrt(2.0 / math.pi)
    half = 0.5 * x
    return (half + half * jnp.tanh(x * (x * x * (c * 0.044715) + c))).astype(bf16)


def head_windows(heads, head_dim):
    out = []
    for h in range(heads):
        lo = h * head_dim
        base = lo // LANES * LANES
        out.append((lo, base, LANES if lo + head_dim <= base + LANES else 2 * LANES))
    return out


def attention(qkv, a_ref, cap_ref, heads, head_dim):
    width = heads * head_dim
    scale = head_dim ** -0.5 * math.log2(math.e)
    wins = head_windows(heads, head_dim)

    def lanes(h):
        _, base, w = wins[h]
        return lax.broadcasted_iota(jnp.int32, (1, w), 1) + base

    def scores(h):
        lo, base, w = wins[h]
        lane = lanes(h)
        own = jnp.where((lane >= lo) & (lane < lo + head_dim), 1.0, 0.0).astype(bf16)
        q = qkv[:, base:base + w] * own
        k = qkv[:, width + base:width + base + w]
        return lax.dot_general(q, k, (((1,), (1,)), ((), ())), preferred_element_type=f32)

    ahead = scores(0)
    for h in range(heads):
        s, ahead = ahead, scores(h + 1) if h + 1 < heads else None
        lo, base, w = wins[h]
        s = jnp.minimum(s * scale, cap_ref[...])
        e = jnp.exp2(s - jnp.max(s, -1, keepdims=True))
        p = (e * (1.0 / jnp.sum(e, -1, keepdims=True))).astype(bf16)
        o = project(p, qkv[:, 2 * width + base:2 * width + base + w])
        if lo != base:
            o = jnp.where(jnp.broadcast_to(lanes(h) >= lo, o.shape), o, a_ref[:, base:base + w])
        a_ref[:, base:base + w] = o


def kernel(n_sp, heads, head_dim, x_hbm, len_ref, norm_ref, wqkv_hbm, wout_hbm, wup_hbm, wdown_hbm, y_hbm,
           wqkv, wout, wup, wdown, xb, qkv, ab, hb, nb, ub, zb, rb, cap,
           w_sem, x_sem, send_sem, recv_sem, y_sem, own_sem):
    videos, frames, rows, width = x_hbm.shape
    steps = videos * frames
    per_dev = rows // n_sp
    per_chunk = rows // (n_sp * frames)
    chunks = per_dev // per_chunk
    half = rows // 2
    me = lax.axis_index("sp")
    peers = n_sp - 1

    barrier = pltpu.get_barrier_semaphore()

    @pl.loop(1, n_sp)
    def _(k):
        pl.semaphore_signal(barrier, inc=1, device_id={"sp": lax.rem(me + k, n_sp)}, device_id_type=MESH)

    weights = ((wqkv_hbm, wqkv), (wout_hbm, wout), (wup_hbm, wup), (wdown_hbm, wdown))

    def load(i, layer):
        return pltpu.make_async_copy(weights[i][0].at[layer], weights[i][1], w_sem.at[i])

    def load_x(s):
        return pltpu.make_async_copy(x_hbm.at[s // frames, s % frames], xb.at[s % 2], x_sem.at[s % 2])

    load_x(0).start()
    for i in range(4):
        load(i, 0).start()
    cap[...] = jnp.full(cap.shape, OPEN, f32)
    pl.semaphore_wait(barrier, peers)

    def send(s, j):
        t = me * frames + s % frames
        return pltpu.make_async_remote_copy(
            src_ref=zb.at[s, pl.ds(j * per_dev, per_dev), :], dst_ref=rb.at[s // frames, t],
            send_sem=send_sem.at[s], recv_sem=recv_sem.at[s // frames], device_id={"sp": j}, device_id_type=MESH)

    def give(c, j, f):
        v, part = c // chunks, c % chunks
        return pltpu.make_async_remote_copy(
            src_ref=zb.at[c, pl.ds((j * frames + f) * per_chunk, per_chunk), :],
            dst_ref=y_hbm.at[v, f, pl.ds(me * per_dev + part * per_chunk, per_chunk), :],
            send_sem=send_sem.at[c], recv_sem=y_sem, device_id={"sp": j}, device_id_type=MESH)

    def keep(c, f):
        v, part = c // chunks, c % chunks
        return pltpu.make_async_copy(
            zb.at[c, pl.ds((me * frames + f) * per_chunk, per_chunk), :],
            y_hbm.at[v, f, pl.ds(me * per_dev + part * per_chunk, per_chunk), :], own_sem)

    def wait_sent(slot):
        sent = zb.at[slot, pl.ds(0, peers * per_dev), :]
        pltpu.make_async_copy(sent, sent, send_sem.at[slot]).wait()

    @pl.loop(0, 2 * steps)
    def _(s):
        spatial = s < steps
        layer = s // steps
        slot = s % steps
        c = s - steps
        xs = xb.at[s % 2]

        @pl.when(spatial)
        def _():
            load_x(s).wait()

        @pl.when(s + 1 < steps)
        def _():
            load_x(s + 1).start()

        @pl.when(jnp.logical_and(s >= steps, slot % chunks == 0))
        def _():
            v = slot // chunks
            got = rb.at[v, pl.ds(0, peers * frames)]
            pltpu.make_async_copy(got, got, recv_sem.at[v]).wait()
            shift = per_chunk.bit_length() - 1
            limit = len_ref[v]
            for r in range(0, rows, LANES):
                qi = lax.broadcasted_iota(jnp.int32, (LANES, rows), 0) + r
                ki = lax.broadcasted_iota(jnp.int32, (LANES, rows), 1)
                kt = lax.shift_right_logical(ki, shift)
                ok = ((qi & (per_chunk - 1)) == (ki & (per_chunk - 1))) & (kt <= lax.shift_right_logical(qi, shift)) & (kt < limit)
                cap[r:r + LANES, :] = jnp.where(ok, OPEN, MASKED)

        @pl.when(s >= steps)
        def _():
            part = slot % chunks
            piece = rb[slot // chunks, :, pl.ds(part * per_chunk, per_chunk), :]
            xs[...] = piece.reshape(rows, width)

        norms = norm_ref[layer].astype(f32)
        for r in range(0, rows, half):
            nb[r:r + half, :] = layer_norm(xs[r:r + half, :], norms[0:1], norms[1:2])

        @pl.when(slot == 0)
        def _():
            load(0, layer).wait()

        qkv[...] = project(nb[...], wqkv[...])

        @pl.when(s == steps - 1)
        def _():
            load(0, 1).start()

        attention(qkv, ab, cap, heads, head_dim)

        @pl.when(slot == 0)
        def _():
            for i in range(1, 4):
                load(i, layer).wait()

        @pl.when(s >= steps)
        def _():
            wait_sent(slot)

        @pl.loop(0, 2)
        def _(m):
            at = pl.ds(pl.multiple_of(m * half, half), half)
            norms = norm_ref[layer].astype(f32)
            hb[...] = residual(xs[at, :], project(ab[at, :], wout[...]))
            nb[at, :] = layer_norm(hb[...], norms[2:3], norms[3:4])
            ub[...] = gelu(project(nb[at, :], wup[...]))
            zb[slot, at, :] = residual(hb[...], project(ub[...], wdown[...]))

        @pl.when(s == steps - 1)
        def _():
            for i in range(1, 4):
                load(i, 1).start()

        @pl.when(spatial)
        def _():
            @pl.loop(1, n_sp)
            def _(k):
                send(s, lax.rem(me + k, n_sp)).start()
            rb[s // frames, me * frames + s % frames] = zb[s, pl.ds(pl.multiple_of(me * per_dev, per_dev), per_dev), :]

        @pl.when(s >= steps)
        def _():
            @pl.loop(1, n_sp)
            def _(k):
                for f in range(frames):
                    give(c, lax.rem(me + k, n_sp), f).start()
            for f in range(frames):
                keep(c, f).start()

    for slot in range(steps):
        wait_sent(slot)
    kept = y_hbm.at[:, :, pl.ds(0, per_dev), :]
    pltpu.make_async_copy(kept, kept, own_sem).wait()
    got = y_hbm.at[:, :, pl.ds(0, peers * per_dev), :]
    pltpu.make_async_copy(got, got, y_sem).wait()


def solution(mesh):
    act_spec = P('data', 'sp', None, None)
    n_sp = mesh.shape['sp']

    def local_step(latents, valid_len, norm_w, w_qkv, w_out, w_up, w_down):
        videos, frames, rows, width = latents.shape
        heads, head_dim = w_out.shape[1:3]
        hidden = w_up.shape[2]
        tokens = videos * frames * rows
        half = rows // 2
        any_spec = pl.BlockSpec(memory_space=pl.ANY)
        dma = pltpu.SemaphoreType.DMA
        steps = videos * frames
        return pl.pallas_call(
            functools.partial(kernel, n_sp, heads, head_dim),
            out_shape=jax.ShapeDtypeStruct(latents.shape, bf16),
            in_specs=[any_spec, pl.BlockSpec(memory_space=pltpu.SMEM), pl.BlockSpec(memory_space=pltpu.VMEM)] + [any_spec] * 4,
            out_specs=any_spec,
            scratch_shapes=[
                pltpu.VMEM((width, 3 * width), bf16), pltpu.VMEM((width, width), bf16),
                pltpu.VMEM((width, hidden), bf16), pltpu.VMEM((hidden, width), bf16),
                pltpu.VMEM((2, rows, width), bf16), pltpu.VMEM((rows, 3 * width), bf16),
                pltpu.VMEM((rows, width), bf16), pltpu.VMEM((half, width), bf16), pltpu.VMEM((rows, width), bf16),
                pltpu.VMEM((half, hidden), bf16), pltpu.VMEM((steps, rows, width), bf16),
                pltpu.VMEM((videos, n_sp * frames, rows // n_sp, width), bf16), pltpu.VMEM((rows, rows), f32),
                dma((4,)), dma((2,)), dma((steps,)), dma((videos,)), dma, dma,
            ],
            compiler_params=pltpu.CompilerParams(collective_id=0, has_side_effects=True, vmem_limit_bytes=66_000_000),
            cost_estimate=pl.CostEstimate(
                flops=2 * 2 * tokens * width * (4 * width + 2 * hidden), bytes_accessed=70_000_000, transcendentals=0),
            name="dit",
        )(latents, valid_len, norm_w, w_qkv, w_out.reshape(2, width, width), w_up, w_down)

    return jax.shard_map(local_step, mesh=mesh, in_specs=(act_spec, P('data'), P(), P(), P(), P(), P()), out_specs=act_spec, check_vma=False)
```

time: 781 us -> 275 us (0.35); the launches traced: 772 us -> 275 us
  matrix products: 326 us -> 0 us
  Pallas kernels: 0 us -> 270 us
  local copies, waits for them, and re-layouts: 169 us -> 4.88 us
  blocking collectives: 116 us -> 0 us
  waiting for transfers between devices: 105 us -> 0 us
  other arithmetic: 41.2 us -> 0 us
  starting transfers between devices: 11.3 us -> 0 us
    dot_general x14 -> x0, matrix products: 282 us -> none  [the longest x8 206 us: project(): jnp.dot(tokens, weight, preferred_element_type=jnp.float32)]
    pallas_call x0 -> x1, Pallas kernels: none -> 270 us  [local_step(): pl.pallas_call(functools.partial(kernel, n_sp, heads, head_dim), out_shap...]
    all_to_all x1 -> x0, blocking collectives: 116 us -> none  [local_step(): return lax.all_to_all(temporal, 'sp', 1, 2, tiled=True)]
    all_to_all x1 -> x0, waiting for transfers between devices: 105 us -> none  [local_step(): by_patch = lax.all_to_all(spatial, 'sp', 2, 1, tiled=True)]
    reshape x2 -> x0, local copies, waits for them, and re-layouts: 57.5 us -> none  [the longest x1 49.4 us: attention(): split_heads = qkv_proj.reshape(lead_shape + (3, num_heads, head_dim))]
    sub x4 -> x0, matrix products: 43.7 us -> none  [one_tile(): attn_prob = jax.nn.softmax(scores, axis=-1).astype(jnp.bfloat16)]
    convert_element_type x5 -> x0, local copies, waits for them, and re-layouts: 42.3 us -> none  [the longest x1 18.7 us: project(): jnp.dot(tokens, weight, preferred_element_type=jnp.float32)]
    slice x2 -> x0, local copies, waits for them, and re-layouts: 21.6 us -> none  [the longest x1 17 us: attention(): value_h = split_heads[..., 2, :, :]]
  transfers between devices with their start and end apart: 1 -> 0, of which waited for: 1 -> 0; matrix products, arithmetic and copies ran while one was open for 0% -> 0% of each run, Pallas kernels for 0% -> 0%
where the time goes in v1:
time: 275 us
  Pallas kernels  270 us (98%)
  local copies, waits for them, and re-layouts  4.88 us (2%)
    pallas_call x1, Pallas kernels, local_step(): pl.pallas_call(functools.partial(kernel, n_sp, heads, head_dim), out_shap...  270 us

profile of v1, /device:TPU:21, one launch (start us, length us, event | category | flops | bytes accessed | tf_op | source)
XLA Modules:
  0.0 275.0 jit_solution(8443599762481463595)
XLA Ops:
  0.0 270.1 %dit.1 = bf16[2,2,512,1152]{3,2,1,0:T(8,128)(2,1)} custom-call(bf16[2,2,512,1152]{3,2,1,0:T(8,128)(2,1)} %x_hbm.1, s32[2]{0:T(128)} %len_ref.1, bf16[2,4,1152]{2,1,0:T(4,128)(2,1)} %norm_ref.1, bf16[2,1152,3456]{2,1,0:T(8,128)(2,1)} %wqkv_hbm.1, bf16[2,1152,1152]{2,1,0:T(8,128)(2,1)} %bitcast.1, bf16[2,1152,4608]{2,1,0:T(8,128)(2,1)} %wup_hbm.1, ...), custom_call_target="tpu_custom_call" | custom-call | flops 130459631616 | bytes 70000000 | tf_op jit(solution)/shard_map/dit/pallas_call | solution.py:248
  270.1 4.9 %copy.9 = bf16[2,2,512,1152]{3,2,1,0:T(8,128)(2,1)} copy(bf16[2,2,512,1152]{3,2,1,0:T(8,128)(2,1)} %dit.1) | data formatting | bytes 9437184

commit v2 on v1

v2 whole, which is shorter than its diff:
```python
import functools
import math

import jax
import jax.numpy as jnp
from jax import lax
from jax.experimental import pallas as pl
from jax.experimental.pallas import tpu as pltpu
from jax.sharding import PartitionSpec as P

LN_EPS = 1e-6
MASKED = -1e30
OPEN = 3e38
LANES = 128
TILE = 256
SUB = 8
f32, bf16 = jnp.float32, jnp.bfloat16
MESH = pl.DeviceIdType.MESH


def layer_norm(tokens, gain, shift):
    values = tokens.astype(f32)
    inv_width = 1.0 / values.shape[-1]
    centered = values - jnp.sum(values, -1, keepdims=True) * inv_width
    variance = jnp.sum(centered * centered, -1, keepdims=True) * inv_width
    return (centered * lax.rsqrt(variance + LN_EPS) * gain + shift).astype(bf16)


def project(a, b):
    return jnp.dot(a, b, preferred_element_type=f32).astype(bf16)


def residual(base, delta):
    return (base.astype(f32) + delta.astype(f32)).astype(bf16)


def gelu(u):
    x = u.astype(f32)
    c = math.sqrt(2.0 / math.pi)
    half = 0.5 * x
    return (half + half * jnp.tanh(x * (x * x * (c * 0.044715) + c))).astype(bf16)


def head_windows(heads, head_dim):
    out = []
    for h in range(heads):
        lo = h * head_dim
        base = lo // LANES * LANES
        out.append((lo, base, LANES if lo + head_dim <= base + LANES else 2 * LANES))
    return out


def project_and_attend(norm_rows, nb, w, qkv, a_ref, heads, head_dim, groups, look, cap_ref):
    rows, width = nb.shape
    scale = head_dim ** -0.5 * math.log2(math.e)
    wins = head_windows(heads, head_dim)
    size = rows // groups
    piece = rows // 2
    queue = [(h, r) for h in range(heads) for r in range(0, rows, piece)]
    made = set()

    def lanes(h):
        _, base, w_ = wins[h]
        return lax.broadcasted_iota(jnp.int32, (1, w_), 1) + base

    def tiles(h, parts):
        _, base, w_ = wins[h]
        spans = [(p * width + base, p * width + base + w_ - 1) for p in parts]
        return list(dict.fromkeys(t for lo, hi in spans for t in range(lo // TILE, hi // TILE + 1)))

    def make(t, r):
        if (t, r) not in made:
            made.add((t, r))
            cols = slice(t * TILE, min((t + 1) * TILE, 3 * width))
            qkv[r:r + piece, cols] = project(nb[r:r + piece, :], w[:, cols])

    def need(h, parts):
        for t in tiles(h, parts):
            for r in range(0, rows, piece):
                make(t, r)

    order = list(dict.fromkeys(t for h in range(heads) for t in tiles(h, (0, 1, 2))))
    pieces = [(t, r) for t in order for r in range(0, rows, piece)]

    def scores(i):
        h, r = queue[i]
        need(h, (0, 1))
        lo, base, w_ = wins[h]
        lane = lanes(h)
        own = jnp.where((lane >= lo) & (lane < lo + head_dim), 1.0, 0.0).astype(bf16)
        q = qkv[r:r + piece, base:base + w_] * own
        k0 = r // size * size
        k = qkv[k0:k0 + size, width + base:width + base + w_]
        return lax.dot_general(q, k, (((1,), (1,)), ((), ())), preferred_element_type=f32)

    for r in range(0, rows, piece):
        norm_rows(r // piece)
        for t in tiles(0, (0, 1, 2)):
            make(t, r)
    ready = {i: scores(i) for i in range(look)}
    for i, (h, r) in enumerate(queue):
        if i + look < len(queue):
            ready[i + look] = scores(i + look)
        left = [u for u in pieces if u not in made]
        for u in left[:pl.cdiv(len(left), max(1, len(queue) - i - 2 * look))]:
            make(*u)
        need(h, (2,))
        lo, base, w_ = wins[h]
        k0 = r // size * size
        s = ready.pop(i) * scale
        if cap_ref is not None:
            s = jnp.minimum(s, cap_ref[...])
        e = jnp.exp2(s - jnp.max(s, -1, keepdims=True))
        p = (e * (1.0 / jnp.sum(e, -1, keepdims=True))).astype(bf16)
        o = project(p, qkv[k0:k0 + size, 2 * width + base:2 * width + base + w_])
        if lo != base:
            o = jnp.where(jnp.broadcast_to(lanes(h) >= lo, o.shape), o, a_ref[r:r + piece, base:base + w_])
        a_ref[r:r + piece, base:base + w_] = o


def kernel(n_sp, heads, head_dim, x_hbm, len_ref, norm_ref, wqkv_hbm, wout_hbm, wup_hbm, wdown_hbm, y_hbm,
           wqkv, wout, wup, wdown, xb, qkv, ab, hb, nb, ub, zb, rb, cap,
           w_sem, x_sem, send_sem, recv_sem, y_sem, own_sem):
    videos, frames, pairs, _, per_dev, width = x_hbm.shape
    rows = pairs * 2 * per_dev
    steps = videos * frames
    half = rows // 2
    groups = per_dev // SUB
    chunks = groups // 2
    me = lax.axis_index("sp")
    peers = n_sp - 1

    barrier = pltpu.get_barrier_semaphore()

    @pl.loop(1, n_sp)
    def _(k):
        pl.semaphore_signal(barrier, inc=1, device_id={"sp": lax.rem(me + k, n_sp)}, device_id_type=MESH)

    weights = ((wqkv_hbm, wqkv), (wout_hbm, wout), (wup_hbm, wup), (wdown_hbm, wdown))

    def load(i, layer):
        return pltpu.make_async_copy(weights[i][0].at[layer], weights[i][1], w_sem.at[i])

    def load_x(s, m):
        return pltpu.make_async_copy(
            x_hbm.at[s // frames, s % frames, :, m],
            xb.at[s % 2, m], x_sem.at[s % 2, m])

    for m in range(2):
        load_x(0, m).start()
    for i in range(4):
        load(i, 0).start()

    def frame_rows(s):
        return pl.ds(pl.multiple_of((me * frames + s % frames) * SUB, SUB), SUB)

    def send(s, m, pair):
        return pltpu.make_async_remote_copy(
            src_ref=zb.at[s, pl.ds((m * pairs + pair) * groups, groups)],
            dst_ref=rb.at[s // frames, :, frame_rows(s), :],
            send_sem=send_sem.at[s], recv_sem=recv_sem.at[s // frames],
            device_id={"sp": 2 * pair + m}, device_id_type=MESH)

    def result_rows(c, m):
        return pl.ds(pl.multiple_of(me * per_dev + (c % chunks * 2 + m) * SUB, SUB), SUB)

    def give(c, m, j):
        return pltpu.make_async_remote_copy(
            src_ref=zb.at[c, pl.ds((m * n_sp + j) * frames, frames)],
            dst_ref=y_hbm.at[c // chunks, :, result_rows(c, m), :],
            send_sem=send_sem.at[c], recv_sem=y_sem, device_id={"sp": j}, device_id_type=MESH)

    def keep(c, m):
        return pltpu.make_async_copy(
            zb.at[c, pl.ds((m * n_sp + me) * frames, frames)],
            y_hbm.at[c // chunks, :, result_rows(c, m), :], own_sem)

    def wait_sent(slot):
        sent = zb.at[slot, pl.ds(0, peers * groups)]
        pltpu.make_async_copy(sent, sent, send_sem.at[slot]).wait()

    @pl.loop(0, 2 * steps)
    def _(s):
        spatial = s < steps
        layer = s // steps
        slot = s % steps
        xs = xb.at[s % 2]

        @pl.when(spatial)
        def _():
            for m in range(2):
                load_x(s, m).wait()

        @pl.when(s + 1 < steps)
        def _():
            for m in range(2):
                load_x(s + 1, m).start()

        @pl.when(jnp.logical_and(s >= steps, slot % chunks == 0))
        def _():
            v = slot // chunks
            got = rb.at[v, :, pl.ds(0, peers * frames * SUB), :]
            pltpu.make_async_copy(got, got, recv_sem.at[v]).wait()
            shift = SUB.bit_length() - 1
            limit = len_ref[v]
            for r in range(0, half, LANES):
                qi = lax.broadcasted_iota(jnp.int32, (LANES, half), 0) + r
                ki = lax.broadcasted_iota(jnp.int32, (LANES, half), 1)
                kt = lax.shift_right_logical(ki, shift)
                ok = ((qi & (SUB - 1)) == (ki & (SUB - 1))) & (kt <= lax.shift_right_logical(qi, shift)) & (kt < limit)
                cap[r:r + LANES, :] = jnp.where(ok, OPEN, MASKED)

        @pl.when(slot == 0)
        def _():
            load(0, layer).wait()

        def norm_rows(m):
            norms = norm_ref[layer].astype(f32)
            nb[m * half:(m + 1) * half, :] = layer_norm(xs[m].reshape(half, width), norms[0:1], norms[1:2])

        @pl.when(spatial)
        def _():
            project_and_attend(norm_rows, nb, wqkv, qkv, ab, heads, head_dim, 1, 3, None)

        @pl.when(s >= steps)
        def _():
            for m in range(2):
                xs[m] = rb[slot // chunks, slot % chunks * 2 + m].reshape(pairs, per_dev, width)
            project_and_attend(norm_rows, nb, wqkv, qkv, ab, heads, head_dim, 2, 2, cap)

        @pl.when(s == steps - 1)
        def _():
            load(0, 1).start()

        @pl.when(slot == 0)
        def _():
            for i in range(1, 4):
                load(i, layer).wait()

        @pl.when(s >= steps)
        def _():
            wait_sent(slot)

        @pl.loop(0, 2)
        def _(m):
            at = pl.ds(pl.multiple_of(m * half, half), half)
            norms = norm_ref[layer].astype(f32)
            hb[...] = residual(xs[m].reshape(half, width), project(ab[at, :], wout[...]))
            nb[at, :] = layer_norm(hb[...], norms[2:3], norms[3:4])
            ub[...] = gelu(project(nb[at, :], wup[...]))
            z = residual(hb[...], project(ub[...], wdown[...]))
            zb[slot, pl.ds(m * (half // SUB), half // SUB)] = z.reshape(half // SUB, SUB, width)

            @pl.when(jnp.logical_and(s == 0, m == 0))
            def _():
                pl.semaphore_wait(barrier, peers)

            @pl.when(spatial)
            def _():
                @pl.loop(0, pairs)
                def _(k):
                    pair = lax.rem(me // 2 + k, pairs)

                    @pl.when(2 * pair + m != me)
                    def _():
                        send(s, m, pair).start()

                @pl.when(m == me % 2)
                def _():
                    for g in range(groups):
                        rb[s // frames, g, frame_rows(s), :] = zb[s, (m * pairs + me // 2) * groups + g]

            @pl.when(s >= steps)
            def _():
                @pl.loop(1, n_sp)
                def _(k):
                    give(slot, m, lax.rem(me + k, n_sp)).start()
                keep(slot, m).start()

        @pl.when(s == steps - 1)
        def _():
            for i in range(1, 4):
                load(i, 1).start()

    for slot in range(steps):
        wait_sent(slot)
    kept = y_hbm.at[:, :, pl.ds(0, per_dev), :]
    pltpu.make_async_copy(kept, kept, own_sem).wait()
    got = y_hbm.at[:, :, pl.ds(0, peers * per_dev), :]
    pltpu.make_async_copy(got, got, y_sem).wait()


def solution(mesh):
    act_spec = P('data', 'sp', None, None)
    n_sp = mesh.shape['sp']

    def local_step(latents, valid_len, norm_w, w_qkv, w_out, w_up, w_down):
        videos, frames, rows, width = latents.shape
        heads, head_dim = w_out.shape[1:3]
        hidden = w_up.shape[2]
        tokens = videos * frames * rows
        half = rows // 2
        any_spec = pl.BlockSpec(memory_space=pl.ANY)
        dma = pltpu.SemaphoreType.DMA
        steps = videos * frames
        return pl.pallas_call(
            functools.partial(kernel, n_sp, heads, head_dim),
            out_shape=jax.ShapeDtypeStruct(latents.shape, bf16),
            in_specs=[any_spec, pl.BlockSpec(memory_space=pltpu.SMEM), pl.BlockSpec(memory_space=pltpu.VMEM)] + [any_spec] * 4,
            out_specs=any_spec,
            scratch_shapes=[
                pltpu.VMEM((width, 3 * width), bf16), pltpu.VMEM((width, width), bf16),
                pltpu.VMEM((width, hidden), bf16), pltpu.VMEM((hidden, width), bf16),
                pltpu.VMEM((2, 2, n_sp // 2, rows // n_sp, width), bf16), pltpu.VMEM((rows, 3 * width), bf16),
                pltpu.VMEM((rows, width), bf16), pltpu.VMEM((half, width), bf16), pltpu.VMEM((rows, width), bf16),
                pltpu.VMEM((half, hidden), bf16), pltpu.VMEM((steps, rows // SUB, SUB, width), bf16),
                pltpu.VMEM((videos, rows // n_sp // SUB, n_sp * frames * SUB, width), bf16), pltpu.VMEM((half, half), f32),
                dma((4,)), dma((2, 2)), dma((steps,)), dma((videos,)), dma, dma,
            ],
            compiler_params=pltpu.CompilerParams(collective_id=0, has_side_effects=True, vmem_limit_bytes=66_000_000),
            cost_estimate=pl.CostEstimate(
                flops=2 * 2 * tokens * width * (4 * width + 2 * hidden), bytes_accessed=70_000_000, transcendentals=0),
            name="dit",
        )(latents.reshape(videos, frames, n_sp // 2, 2, rows // n_sp, width), valid_len, norm_w, w_qkv, w_out.reshape(2, width, width), w_up, w_down)

    return jax.shard_map(local_step, mesh=mesh, in_specs=(act_spec, P('data'), P(), P(), P(), P(), P()), out_specs=act_spec, check_vma=False)
```

time: 275 us -> 252 us (0.916)
  Pallas kernels: 270 us -> 247 us
    pallas_call x1, Pallas kernels: 270 us -> 247 us  [local_step(): pl.pallas_call(functools.partial(kernel, n_sp, heads, head_dim), out_shap...]
where the time goes in v2:
time: 252 us
  Pallas kernels  247 us (98%)
  local copies, waits for them, and re-layouts  4.88 us (2%)
    pallas_call x1, Pallas kernels, local_step(): pl.pallas_call(functools.partial(kernel, n_sp, heads, head_dim), out_shap...  247 us

profile of v2, /device:TPU:21, one launch (start us, length us, event | category | flops | bytes accessed | tf_op | source)
XLA Modules:
  0.0 252.2 jit_solution(10060269399450134495)
XLA Ops:
  0.0 247.3 %dit.1 = bf16[2,2,512,1152]{3,2,1,0:T(8,128)(2,1)} custom-call(bf16[2,2,8,2,32,1152]{5,4,3,2,1,0:T(8,128)(2,1)} %bitcast.3, s32[2]{0:T(128)} %len_ref.1, bf16[2,4,1152]{2,1,0:T(4,128)(2,1)} %norm_ref.1, bf16[2,1152,3456]{2,1,0:T(8,128)(2,1)} %wqkv_hbm.1, bf16[2,1152,1152]{2,1,0:T(8,128)(2,1)} %bitcast.2, bf16[2,1152,4608]{2,1,0:T(8,128)(2,1)} %wup_hbm.1, ...), custom_call_target="tpu_custom_call" | custom-call | flops 130459631616 | bytes 70000000 | tf_op jit(solution)/shard_map/dit/pallas_call | solution.py:306
  247.3 4.9 %copy.9 = bf16[2,2,512,1152]{3,2,1,0:T(8,128)(2,1)} copy(bf16[2,2,512,1152]{3,2,1,0:T(8,128)(2,1)} %dit.1) | data formatting | bytes 9437184

commit v3 on v2

--- a/solution.py
+++ b/solution.py
@@ -118,9 +118,9 @@
         a_ref[r:r + piece, base:base + w_] = o
 
 
-def kernel(n_sp, heads, head_dim, x_hbm, len_ref, norm_ref, wqkv_hbm, wout_hbm, wup_hbm, wdown_hbm, y_hbm,
+def kernel(n_sp, heads, head_dim, x_hbm, len_ref, norm_ref, wqkv_hbm, wout_hbm, wup_hbm, wdown_hbm, y_ref,
            wqkv, wout, wup, wdown, xb, qkv, ab, hb, nb, ub, zb, rb, cap,
-           w_sem, x_sem, send_sem, recv_sem, y_sem, own_sem):
+           w_sem, x_sem, send_sem, recv_sem, y_sem):
     videos, frames, pairs, _, per_dev, width = x_hbm.shape
     rows = pairs * 2 * per_dev
     steps = videos * frames
@@ -167,13 +167,8 @@
     def give(c, m, j):
         return pltpu.make_async_remote_copy(
             src_ref=zb.at[c, pl.ds((m * n_sp + j) * frames, frames)],
-            dst_ref=y_hbm.at[c // chunks, :, result_rows(c, m), :],
+            dst_ref=y_ref.at[c // chunks, :, result_rows(c, m), :],
             send_sem=send_sem.at[c], recv_sem=y_sem, device_id={"sp": j}, device_id_type=MESH)
-
-    def keep(c, m):
-        return pltpu.make_async_copy(
-            zb.at[c, pl.ds((m * n_sp + me) * frames, frames)],
-            y_hbm.at[c // chunks, :, result_rows(c, m), :], own_sem)
 
     def wait_sent(slot):
         sent = zb.at[slot, pl.ds(0, peers * groups)]
@@ -275,7 +270,8 @@
                 @pl.loop(1, n_sp)
                 def _(k):
                     give(slot, m, lax.rem(me + k, n_sp)).start()
-                keep(slot, m).start()
+                for f in range(frames):
+                    y_ref[slot // chunks, f, result_rows(slot, m), :] = zb[slot, (m * n_sp + me) * frames + f]
 
         @pl.when(s == steps - 1)
         def _():
@@ -284,9 +280,7 @@
 
     for slot in range(steps):
         wait_sent(slot)
-    kept = y_hbm.at[:, :, pl.ds(0, per_dev), :]
-    pltpu.make_async_copy(kept, kept, own_sem).wait()
-    got = y_hbm.at[:, :, pl.ds(0, peers * per_dev), :]
+    got = y_ref.at[:, :, pl.ds(0, peers * per_dev), :]
     pltpu.make_async_copy(got, got, y_sem).wait()
 
 
@@ -305,9 +299,9 @@
         steps = videos * frames
         return pl.pallas_call(
             functools.partial(kernel, n_sp, heads, head_dim),
-            out_shape=jax.ShapeDtypeStruct(latents.shape, bf16),
+            out_shape=pltpu.VMEM(latents.shape, bf16),
             in_specs=[any_spec, pl.BlockSpec(memory_space=pltpu.SMEM), pl.BlockSpec(memory_space=pltpu.VMEM)] + [any_spec] * 4,
-            out_specs=any_spec,
+            out_specs=pl.BlockSpec(memory_space=pltpu.VMEM),
             scratch_shapes=[
                 pltpu.VMEM((width, 3 * width), bf16), pltpu.VMEM((width, width), bf16),
                 pltpu.VMEM((width, hidden), bf16), pltpu.VMEM((hidden, width), bf16),
@@ -315,9 +309,9 @@
                 pltpu.VMEM((rows, width), bf16), pltpu.VMEM((half, width), bf16), pltpu.VMEM((rows, width), bf16),
                 pltpu.VMEM((half, hidden), bf16), pltpu.VMEM((steps, rows // SUB, SUB, width), bf16),
                 pltpu.VMEM((videos, rows // n_sp // SUB, n_sp * frames * SUB, width), bf16), pltpu.VMEM((half, half), f32),
-                dma((4,)), dma((2, 2)), dma((steps,)), dma((videos,)), dma, dma,
+                dma((4,)), dma((2, 2)), dma((steps,)), dma((videos,)), dma,
             ],
-            compiler_params=pltpu.CompilerParams(collective_id=0, has_side_effects=True, vmem_limit_bytes=66_000_000),
+            compiler_params=pltpu.CompilerParams(collective_id=0, has_side_effects=True, vmem_limit_bytes=62_000_000),
             cost_estimate=pl.CostEstimate(
                 flops=2 * 2 * tokens * width * (4 * width + 2 * hidden), bytes_accessed=70_000_000, transcendentals=0),
             name="dit",

time: 252 us -> 251 us (level)
  local copies, waits for them, and re-layouts: 4.88 us -> 2.19 us
    unnamed x1, local copies, waits for them, and re-layouts: 4.88 us -> 2.19 us
where the time goes in v3:
time: 251 us
  Pallas kernels  249 us (99%)
    pallas_call x1, Pallas kernels, local_step(): pl.pallas_call(functools.partial(kernel, n_sp, heads, head_dim), out_shap...  249 us

profile of v3, /device:TPU:21, one launch (start us, length us, event | category | flops | bytes accessed | tf_op | source)
XLA Modules:
  0.0 250.8 jit_solution(10649263577217572250)
XLA Ops:
  0.0 248.6 %dit.1 = bf16[2,2,512,1152]{3,2,1,0:T(8,128)(2,1)S(1)} custom-call(bf16[2,2,8,2,32,1152]{5,4,3,2,1,0:T(8,128)(2,1)} %bitcast.3, s32[2]{0:T(128)} %len_ref.1, bf16[2,4,1152]{2,1,0:T(4,128)(2,1)} %norm_ref.1, bf16[2,1152,3456]{2,1,0:T(8,128)(2,1)} %wqkv_hbm.1, bf16[2,1152,1152]{2,1,0:T(8,128)(2,1)} %bitcast.2, bf16[2,1152,4608]{2,1,0:T(8,128)(2,1)} %wup_hbm.1, ...), custom_call_target="tpu_custom_call" | custom-call | flops 130459631616 | bytes 70000000 | tf_op jit(solution)/shard_map/dit/pallas_call | solution.py:300
  248.6 2.2 copy.9

commit v4 on v3

--- a/solution.py
+++ b/solution.py
@@ -50,29 +50,35 @@
     return out
 
 
-def project_and_attend(norm_rows, nb, w, qkv, a_ref, heads, head_dim, groups, look, cap_ref):
-    rows, width = nb.shape
+def column_tiles(wins, h, parts, width):
+    _, base, w = wins[h]
+    spans = [(p * width + base, p * width + base + w - 1) for p in parts]
+    return list(dict.fromkeys(t for lo, hi in spans for t in range(lo // TILE, hi // TILE + 1)))
+
+
+def columns(t, width):
+    return slice(t * TILE, min((t + 1) * TILE, 3 * width))
+
+
+def project_and_attend(nb, w, qkv, a_ref, heads, head_dim, groups, look, cap_ref):
+    rows, width = 2 * nb.shape[1], nb.shape[2]
     scale = head_dim ** -0.5 * math.log2(math.e)
     wins = head_windows(heads, head_dim)
     size = rows // groups
     piece = rows // 2
     queue = [(h, r) for h in range(heads) for r in range(0, rows, piece)]
-    made = set()
-
     def lanes(h):
         _, base, w_ = wins[h]
         return lax.broadcasted_iota(jnp.int32, (1, w_), 1) + base
 
-    def tiles(h, parts):
-        _, base, w_ = wins[h]
-        spans = [(p * width + base, p * width + base + w_ - 1) for p in parts]
-        return list(dict.fromkeys(t for lo, hi in spans for t in range(lo // TILE, hi // TILE + 1)))
+    tiles = functools.partial(column_tiles, wins, width=width)
+    made = {(t, r) for t in tiles(0, (0, 1, 2)) for r in range(0, rows, piece)}
 
     def make(t, r):
         if (t, r) not in made:
             made.add((t, r))
-            cols = slice(t * TILE, min((t + 1) * TILE, 3 * width))
-            qkv[r:r + piece, cols] = project(nb[r:r + piece, :], w[:, cols])
+            cols = columns(t, width)
+            qkv[r:r + piece, cols] = project(nb[r // piece], w[:, cols])
 
     def need(h, parts):
         for t in tiles(h, parts):
@@ -93,10 +99,6 @@
         k = qkv[k0:k0 + size, width + base:width + base + w_]
         return lax.dot_general(q, k, (((1,), (1,)), ((), ())), preferred_element_type=f32)
 
-    for r in range(0, rows, piece):
-        norm_rows(r // piece)
-        for t in tiles(0, (0, 1, 2)):
-            make(t, r)
     ready = {i: scores(i) for i in range(look)}
     for i, (h, r) in enumerate(queue):
         if i + look < len(queue):
@@ -119,8 +121,8 @@
 
 
 def kernel(n_sp, heads, head_dim, x_hbm, len_ref, norm_ref, wqkv_hbm, wout_hbm, wup_hbm, wdown_hbm, y_ref,
-           wqkv, wout, wup, wdown, xb, qkv, ab, hb, nb, ub, zb, rb, cap,
-           w_sem, x_sem, send_sem, recv_sem, y_sem):
+           wqkv, wfirst, wout, wup, wdown, xb, qkv, ab, hb, n1, n2, ub, zb, rb, cap,
+           w_sem, first_sem, x_sem, send_sem, recv_sem, y_sem):
     videos, frames, pairs, _, per_dev, width = x_hbm.shape
     rows = pairs * 2 * per_dev
     steps = videos * frames
@@ -146,10 +148,28 @@
             x_hbm.at[s // frames, s % frames, :, m],
             xb.at[s % 2, m], x_sem.at[s % 2, m])
 
+    first = column_tiles(head_windows(heads, head_dim), 0, (0, 1, 2), width)
+
+    def load_first(i, layer):
+        return pltpu.make_async_copy(
+            wqkv_hbm.at[layer, :, pl.ds(first[i] * TILE, TILE)], wfirst.at[i], first_sem.at[i])
+
+    def norm_next(layer, s, m):
+        norms = norm_ref[layer].astype(f32)
+        n1[m] = layer_norm(xb[s % 2, m].reshape(half, width), norms[0:1], norms[1:2])
+
+    def project_first(m):
+        for i, t in enumerate(first):
+            qkv[pl.ds(pl.multiple_of(m * half, half), half), columns(t, width)] = project(n1[m], wfirst[i])
+
     for m in range(2):
         load_x(0, m).start()
+    for i in range(len(first)):
+        load_first(i, 0).start()
     for i in range(4):
         load(i, 0).start()
+    for m in range(2):
+        load_x(1, m).start()
 
     def frame_rows(s):
         return pl.ds(pl.multiple_of((me * frames + s % frames) * SUB, SUB), SUB)
@@ -174,6 +194,15 @@
         sent = zb.at[slot, pl.ds(0, peers * groups)]
         pltpu.make_async_copy(sent, sent, send_sem.at[slot]).wait()
 
+    for m in range(2):
+        load_x(0, m).wait()
+    for i in range(len(first)):
+        load_first(i, 0).wait()
+    for m in range(2):
+        norm_next(0, 0, m)
+        project_first(m)
+    load(0, 0).wait()
+
     @pl.loop(0, 2 * steps)
     def _(s):
         spatial = s < steps
@@ -183,49 +212,17 @@
 
         @pl.when(spatial)
         def _():
-            for m in range(2):
-                load_x(s, m).wait()
-
-        @pl.when(s + 1 < steps)
-        def _():
-            for m in range(2):
-                load_x(s + 1, m).start()
-
-        @pl.when(jnp.logical_and(s >= steps, slot % chunks == 0))
-        def _():
-            v = slot // chunks
-            got = rb.at[v, :, pl.ds(0, peers * frames * SUB), :]
-            pltpu.make_async_copy(got, got, recv_sem.at[v]).wait()
-            shift = SUB.bit_length() - 1
-            limit = len_ref[v]
-            for r in range(0, half, LANES):
-                qi = lax.broadcasted_iota(jnp.int32, (LANES, half), 0) + r
-                ki = lax.broadcasted_iota(jnp.int32, (LANES, half), 1)
-                kt = lax.shift_right_logical(ki, shift)
-                ok = ((qi & (SUB - 1)) == (ki & (SUB - 1))) & (kt <= lax.shift_right_logical(qi, shift)) & (kt < limit)
-                cap[r:r + LANES, :] = jnp.where(ok, OPEN, MASKED)
-
-        @pl.when(slot == 0)
-        def _():
-            load(0, layer).wait()
-
-        def norm_rows(m):
-            norms = norm_ref[layer].astype(f32)
-            nb[m * half:(m + 1) * half, :] = layer_norm(xs[m].reshape(half, width), norms[0:1], norms[1:2])
-
-        @pl.when(spatial)
-        def _():
-            project_and_attend(norm_rows, nb, wqkv, qkv, ab, heads, head_dim, 1, 3, None)
+            project_and_attend(n1, wqkv, qkv, ab, heads, head_dim, 1, 3, None)
 
         @pl.when(s >= steps)
         def _():
-            for m in range(2):
-                xs[m] = rb[slot // chunks, slot % chunks * 2 + m].reshape(pairs, per_dev, width)
-            project_and_attend(norm_rows, nb, wqkv, qkv, ab, heads, head_dim, 2, 2, cap)
+            project_and_attend(n1, wqkv, qkv, ab, heads, head_dim, 2, 2, cap)
 
         @pl.when(s == steps - 1)
         def _():
             load(0, 1).start()
+            for i in range(len(first)):
+                load_first(i, 1).wait()
 
         @pl.when(slot == 0)
         def _():
@@ -235,14 +232,42 @@
         @pl.when(s >= steps)
         def _():
             wait_sent(slot)
+
+        @pl.when(s + 1 < steps)
+        def _():
+            for m in range(2):
+                load_x(s + 1, m).wait()
+
+        @pl.when(jnp.logical_and(s + 1 >= steps, s + 1 < 2 * steps))
+        def _():
+            c = s + 1 - steps
+
+            @pl.when(c % chunks == 0)
+            def _():
+                v = c // chunks
+                got = rb.at[v, :, pl.ds(0, peers * frames * SUB), :]
+                pltpu.make_async_copy(got, got, recv_sem.at[v]).wait()
+                shift = SUB.bit_length() - 1
+                limit = len_ref[v]
+                for r in range(0, half, LANES):
+                    qi = lax.broadcasted_iota(jnp.int32, (LANES, half), 0) + r
+                    ki = lax.broadcasted_iota(jnp.int32, (LANES, half), 1)
+                    kt = lax.shift_right_logical(ki, shift)
+                    ok = ((qi & (SUB - 1)) == (ki & (SUB - 1))) & (kt <= lax.shift_right_logical(qi, shift)) & (kt < limit)
+                    cap[r:r + LANES, :] = jnp.where(ok, OPEN, MASKED)
+
+            for m in range(2):
+                xb[(s + 1) % 2, m] = rb[c // chunks, c % chunks * 2 + m].reshape(pairs, per_dev, width)
 
         @pl.loop(0, 2)
         def _(m):
             at = pl.ds(pl.multiple_of(m * half, half), half)
             norms = norm_ref[layer].astype(f32)
+            norm_next((s + 1) % (2 * steps) // steps, s + 1, m)
             hb[...] = residual(xs[m].reshape(half, width), project(ab[at, :], wout[...]))
-            nb[at, :] = layer_norm(hb[...], norms[2:3], norms[3:4])
-            ub[...] = gelu(project(nb[at, :], wup[...]))
+            project_first(m)
+            n2[...] = layer_norm(hb[...], norms[2:3], norms[3:4])
+            ub[...] = gelu(project(n2[...], wup[...]))
             z = residual(hb[...], project(ub[...], wdown[...]))
             zb[slot, pl.ds(m * (half // SUB), half // SUB)] = z.reshape(half // SUB, SUB, width)
 
@@ -275,8 +300,19 @@
 
         @pl.when(s == steps - 1)
         def _():
+            load(0, 1).wait()
             for i in range(1, 4):
                 load(i, 1).start()
+
+        @pl.when(s == steps - 2)
+        def _():
+            for i in range(len(first)):
+                load_first(i, 1).start()
+
+        @pl.when(s + 2 < steps)
+        def _():
+            for m in range(2):
+                load_x(s + 2, m).start()
 
     for slot in range(steps):
         wait_sent(slot)
@@ -297,19 +333,22 @@
         any_spec = pl.BlockSpec(memory_space=pl.ANY)
         dma = pltpu.SemaphoreType.DMA
         steps = videos * frames
+        firsts = len(column_tiles(head_windows(heads, head_dim), 0, (0, 1, 2), width))
         return pl.pallas_call(
             functools.partial(kernel, n_sp, heads, head_dim),
             out_shape=pltpu.VMEM(latents.shape, bf16),
             in_specs=[any_spec, pl.BlockSpec(memory_space=pltpu.SMEM), pl.BlockSpec(memory_space=pltpu.VMEM)] + [any_spec] * 4,
             out_specs=pl.BlockSpec(memory_space=pltpu.VMEM),
             scratch_shapes=[
-                pltpu.VMEM((width, 3 * width), bf16), pltpu.VMEM((width, width), bf16),
+                pltpu.VMEM((width, 3 * width), bf16), pltpu.VMEM((firsts, width, TILE), bf16),
+                pltpu.VMEM((width, width), bf16),
                 pltpu.VMEM((width, hidden), bf16), pltpu.VMEM((hidden, width), bf16),
                 pltpu.VMEM((2, 2, n_sp // 2, rows // n_sp, width), bf16), pltpu.VMEM((rows, 3 * width), bf16),
-                pltpu.VMEM((rows, width), bf16), pltpu.VMEM((half, width), bf16), pltpu.VMEM((rows, width), bf16),
+                pltpu.VMEM((rows, width), bf16), pltpu.VMEM((half, width), bf16),
+                pltpu.VMEM((2, half, width), bf16), pltpu.VMEM((half, width), bf16),
                 pltpu.VMEM((half, hidden), bf16), pltpu.VMEM((steps, rows // SUB, SUB, width), bf16),
                 pltpu.VMEM((videos, rows // n_sp // SUB, n_sp * frames * SUB, width), bf16), pltpu.VMEM((half, half), f32),
-                dma((4,)), dma((2, 2)), dma((steps,)), dma((videos,)), dma,
+                dma((4,)), dma((firsts,)), dma((2, 2)), dma((steps,)), dma((videos,)), dma,
             ],
             compiler_params=pltpu.CompilerParams(collective_id=0, has_side_effects=True, vmem_limit_bytes=62_000_000),
             cost_estimate=pl.CostEstimate(

time: 251 us -> 246 us (0.980)
  Pallas kernels: 249 us -> 244 us
    pallas_call x1, Pallas kernels: 249 us -> 244 us  [local_step(): pl.pallas_call(functools.partial(kernel, n_sp, heads, head_dim), out_shap...]
where the time goes in v4:
time: 246 us
  Pallas kernels  244 us (99%)
    pallas_call x1, Pallas kernels, local_step(): pl.pallas_call(functools.partial(kernel, n_sp, heads, head_dim), out_shap...  244 us

profile of v4, /device:TPU:21, one launch (start us, length us, event | category | flops | bytes accessed | tf_op | source)
XLA Modules:
  0.0 246.0 jit_solution(17901534844770002884)
XLA Ops:
  0.0 243.8 %dit.1 = bf16[2,2,512,1152]{3,2,1,0:T(8,128)(2,1)S(1)} custom-call(bf16[2,2,8,2,32,1152]{5,4,3,2,1,0:T(8,128)(2,1)} %bitcast.3, s32[2]{0:T(128)} %len_ref.1, bf16[2,4,1152]{2,1,0:T(4,128)(2,1)} %norm_ref.1, bf16[2,1152,3456]{2,1,0:T(8,128)(2,1)} %wqkv_hbm.1, bf16[2,1152,1152]{2,1,0:T(8,128)(2,1)} %bitcast.2, bf16[2,1152,4608]{2,1,0:T(8,128)(2,1)} %wup_hbm.1, ...), custom_call_target="tpu_custom_call" | custom-call | flops 130459631616 | bytes 70000000 | tf_op jit(solution)/shard_map/dit/pallas_call | solution.py:337
  243.8 2.2 copy.9

commit v5 on v4

v5 whole, which is shorter than its diff:
```python
import functools
import math

import jax
import jax.numpy as jnp
from jax import lax
from jax.experimental import pallas as pl
from jax.experimental.pallas import tpu as pltpu
from jax.sharding import PartitionSpec as P

LN_EPS = 1e-6
MASKED = -1e30
OPEN = 3e38
LANES = 128
TILE = 256
SUB = 8
PACK = 16
f32, bf16 = jnp.float32, jnp.bfloat16
MESH = pl.DeviceIdType.MESH


def layer_norm(tokens, gain, shift):
    values = tokens.astype(f32)
    inv_width = 1.0 / values.shape[-1]
    centered = values - jnp.sum(values, -1, keepdims=True) * inv_width
    variance = jnp.sum(centered * centered, -1, keepdims=True) * inv_width
    return (centered * lax.rsqrt(variance + LN_EPS) * gain + shift).astype(bf16)


def project(a, b):
    return jnp.dot(a, b, preferred_element_type=f32).astype(bf16)


def residual(base, delta):
    return (base.astype(f32) + delta.astype(f32)).astype(bf16)


def gelu(u):
    x = u.astype(f32)
    c = math.sqrt(2.0 / math.pi)
    half = 0.5 * x
    return (half + half * jnp.tanh(x * (x * x * (c * 0.044715) + c))).astype(bf16)


def head_windows(heads, head_dim):
    out = []
    for h in range(heads):
        lo = h * head_dim
        base = lo // LANES * LANES
        out.append((lo, base, LANES if lo + head_dim <= base + LANES else 2 * LANES))
    return out


def column_tiles(wins, h, parts, width):
    _, base, w = wins[h]
    spans = [(p * width + base, p * width + base + w - 1) for p in parts]
    return list(dict.fromkeys(t for lo, hi in spans for t in range(lo // TILE, hi // TILE + 1)))


def columns(t, width):
    return slice(t * TILE, min((t + 1) * TILE, 3 * width))


def attend(nb, w_of, qk, vt, a_ref, heads, head_dim, mine, key_halves, made, look, lead, cap_ref):
    _, half, width = nb.shape
    scale = head_dim ** -0.5 * math.log2(math.e)
    wins = head_windows(heads, head_dim)
    made = set(made)
    key_rows = slice(key_halves[0] * half, (key_halves[-1] + 1) * half)

    def pieces(h, parts):
        return [(t, r) for p in parts for t in column_tiles(wins, h, (p,), width) for r in ((mine,) if p == 0 else key_halves)]

    def make(t, r):
        if (t, r) not in made:
            made.add((t, r))
            project_piece(nb, w_of(t), qk, vt, t, r)

    def keys(cols):
        return jnp.concatenate([qk[r, :, cols] for r in key_halves], axis=0)

    def scores(h):
        for u in pieces(h, (0, 1)):
            make(*u)
        lo, base, w_ = wins[h]
        lane = lax.broadcasted_iota(jnp.int32, (1, w_), 1) + base
        own = jnp.where((lane >= lo) & (lane < lo + head_dim), 1.0, 0.0).astype(bf16)
        q = qk[mine, :, base:base + w_] * own
        k = keys(slice(width + base, width + base + w_))
        return lax.dot_general(k, q, (((1,), (1,)), ((), ())), preferred_element_type=f32)

    due = []
    for h in range(heads):
        for p, step in ((0, h - look), (1, h - look), (2, h)):
            due += [(max(step, -1), u) for u in pieces(h, (p,))]
    ready = {h: scores(h) for h in range(look)}
    done, parts = 0, []
    for h in range(heads):
        for step, u in sorted(due, key=lambda d: d[0]):
            if step <= h + lead:
                make(*u)
        if h + look < heads:
            ready[h + look] = scores(h + look)
        s = ready.pop(h)
        if cap_ref is not None:
            s = jnp.minimum(s, cap_ref[...])
        e = jnp.exp2((s - jnp.max(s, 0, keepdims=True)) * scale)
        p = (e * (1.0 / jnp.sum(e, 0, keepdims=True))).astype(bf16)
        lo = h * head_dim
        r0, r1 = lo // PACK * PACK, pl.cdiv(lo + head_dim, PACK) * PACK
        o = jnp.dot(vt[r0:r1, key_rows], p, preferred_element_type=f32)
        parts.append((lo, o[lo - r0:lo - r0 + head_dim, :]))
        while (done + 1) * LANES <= lo + head_dim:
            g0, g1 = done * LANES, (done + 1) * LANES
            rows = [x[max(g0 - l, 0):min(g1 - l, head_dim), :] for l, x in parts if l < g1]
            a_ref[:, g0:g1] = jnp.concatenate(rows, axis=0).astype(bf16).T
            parts = [(l, x) for l, x in parts if l + head_dim > g1]
            done += 1


def project_piece(nb, w, qk, vt, t, r):
    half, width = nb.shape[1:]
    piece = project(nb[r], w)
    cols = columns(t, width)
    if cols.start < 2 * width:
        qk[r, :, cols] = piece
    else:
        vt[cols.start - 2 * width:cols.stop - 2 * width, r * half:(r + 1) * half] = piece.T


def kernel(n_sp, heads, head_dim, x_hbm, len_ref, norm_ref, wqkv_hbm, wout_hbm, wup_hbm, wdown_hbm, y_ref,
           wrest, wfirst, wout, wup, wdown, xb, qk, vt, ab, hb, n1, ub, zb, rb, cap,
           w_sem, rest_sem, first_sem, x_sem, send_sem, recv_sem, y_sem):
    videos, frames, pairs, _, per_dev, width = x_hbm.shape
    rows = pairs * 2 * per_dev
    steps = videos * frames
    half = rows // 2
    groups = per_dev // SUB
    chunks = groups // 2
    me = lax.axis_index("sp")
    peers = n_sp - 1

    barrier = pltpu.get_barrier_semaphore()

    @pl.loop(1, n_sp)
    def _(k):
        pl.semaphore_signal(barrier, inc=1, device_id={"sp": lax.rem(me + k, n_sp)}, device_id_type=MESH)

    weights = ((wout_hbm, wout), (wup_hbm, wup), (wdown_hbm, wdown))

    def load(i, layer):
        return pltpu.make_async_copy(weights[i][0].at[layer], weights[i][1], w_sem.at[i])

    def load_x(s, m):
        return pltpu.make_async_copy(
            x_hbm.at[s // frames, s % frames, :, m], xb.at[s % 2, m], x_sem.at[s % 2, m])

    tiles = pl.cdiv(3 * width, TILE)
    first = column_tiles(head_windows(heads, head_dim), 0, (0, 1, 2), width)
    rest = [t for t in range(tiles) if t not in first]
    extra = [t for t in range(width // TILE) if t not in first]

    def load_tile(t, layer):
        cols = columns(t, width)
        home, sem = (wfirst.at[first.index(t)], first_sem) if t in first else (wrest.at[rest.index(t)], rest_sem)
        size = cols.stop - cols.start
        return pltpu.make_async_copy(
            wqkv_hbm.at[layer, :, pl.ds(cols.start, size)], home.at[:, pl.ds(0, size)],
            sem.at[(first if t in first else rest).index(t)])

    def w_of(t):
        cols = columns(t, width)
        size = cols.stop - cols.start
        return wfirst[first.index(t)] if t in first else wrest[rest.index(t), :, :size]

    def norm_next(layer, s, m):
        norms = norm_ref[layer].astype(f32)
        n1[m] = layer_norm(xb[s % 2, m].reshape(half, width), norms[0:1], norms[1:2])

    def project_first(m):
        for t in first:
            project_piece(n1, w_of(t), qk, vt, t, m)

    for m in range(2):
        load_x(0, m).start()
    for t in first + rest:
        load_tile(t, 0).start()
    for i in range(3):
        load(i, 0).start()
    for m in range(2):
        load_x(1, m).start()

    def frame_rows(s):
        return pl.ds(pl.multiple_of((me * frames + s % frames) * SUB, SUB), SUB)

    def send(s, m, pair):
        return pltpu.make_async_remote_copy(
            src_ref=zb.at[s, pl.ds((m * pairs + pair) * groups, groups)],
            dst_ref=rb.at[s // frames, :, frame_rows(s), :],
            send_sem=send_sem.at[s], recv_sem=recv_sem.at[s // frames],
            device_id={"sp": 2 * pair + m}, device_id_type=MESH)

    def result_rows(c, m):
        return pl.ds(pl.multiple_of(me * per_dev + (c % chunks * 2 + m) * SUB, SUB), SUB)

    def give(c, m, j):
        return pltpu.make_async_remote_copy(
            src_ref=zb.at[c, pl.ds((m * n_sp + j) * frames, frames)],
            dst_ref=y_ref.at[c // chunks, :, result_rows(c, m), :],
            send_sem=send_sem.at[c], recv_sem=y_sem, device_id={"sp": j}, device_id_type=MESH)

    def wait_sent(slot):
        sent = zb.at[slot, pl.ds(0, peers * groups)]
        pltpu.make_async_copy(sent, sent, send_sem.at[slot]).wait()

    for m in range(2):
        load_x(0, m).wait()
    for t in first:
        load_tile(t, 0).wait()
    for m in range(2):
        norm_next(0, 0, m)
        project_first(m)
    for t in rest:
        load_tile(t, 0).wait()

    @pl.loop(0, 2 * steps)
    def _(s):
        spatial = s < steps
        temporal = s >= steps
        layer = s // steps
        slot = s % steps
        xs = xb.at[s % 2]
        attention = functools.partial(attend, n1, w_of, qk, vt, ab, heads, head_dim)
        there = {(t, r) for t in first for r in range(2)}

        def out(m):
            hb[...] = residual(xs[m].reshape(half, width), project(ab[...], wout[...]))

        def norm():
            norms = norm_ref[layer].astype(f32)
            ab[...] = layer_norm(hb[...], norms[2:3], norms[3:4])

        def up():
            ub[...] = gelu(project(ab[...], wup[...]))

        def down(m):
            z = residual(hb[...], project(ub[...], wdown[...]))
            zb[slot, m * (half // SUB):(m + 1) * (half // SUB)] = z.reshape(half // SUB, SUB, width)

        def deliver(m):
            @pl.when(spatial)
            def _():
                @pl.loop(0, pairs)
                def _(k):
                    pair = lax.rem(me // 2 + k, pairs)

                    @pl.when(2 * pair + m != me)
                    def _():
                        send(s, m, pair).start()

                @pl.when(m == me % 2)
                def _():
                    for g in range(groups):
                        rb[s // frames, g, frame_rows(s), :] = zb[s, (m * pairs + me // 2) * groups + g]

            @pl.when(temporal)
            def _():
                @pl.loop(1, n_sp)
                def _(k):
                    give(slot, m, lax.rem(me + k, n_sp)).start()
                for f in range(frames):
                    y_ref[slot // chunks, f, result_rows(slot, m), :] = zb[slot, (m * n_sp + me) * frames + f]

        @pl.when(spatial)
        def _():
            attention(0, (0, 1), there, 3, 2, None)

        @pl.when(temporal)
        def _():
            attention(0, (0,), there, 3, 3, cap)

        @pl.when(slot == 0)
        def _():
            for i in range(3):
                load(i, layer).wait()

        @pl.when(temporal)
        def _():
            wait_sent(slot)

        out(0)
        for t in extra:
            project_piece(n1, w_of(t), qk, vt, t, 1)
        norm()
        up()
        down(0)

        @pl.when(s == 0)
        def _():
            pl.semaphore_wait(barrier, peers)

        deliver(0)

        @pl.when(spatial)
        def _():
            attention(1, (0, 1), {(t, r) for t in range(tiles) for r in range(2)}, 5, 3, None)

        @pl.when(temporal)
        def _():
            attention(1, (1,), there | {(t, 1) for t in extra}, 4, 3, cap)

        @pl.when(s == steps - 1)
        def _():
            for t in rest:
                load_tile(t, 1).start()
            for t in first:
                load_tile(t, 1).wait()

        @pl.when(s + 1 < steps)
        def _():
            for m in range(2):
                load_x(s + 1, m).wait()

        @pl.when(jnp.logical_and(s + 1 >= steps, s + 1 < 2 * steps))
        def _():
            c = s + 1 - steps

            @pl.when(c % chunks == 0)
            def _():
                v = c // chunks
                got = rb.at[v, :, pl.ds(0, peers * frames * SUB), :]
                pltpu.make_async_copy(got, got, recv_sem.at[v]).wait()
                shift = SUB.bit_length() - 1
                limit = len_ref[v]
                for r in range(0, half, LANES):
                    ki = lax.broadcasted_iota(jnp.int32, (LANES, half), 0) + r
                    qi = lax.broadcasted_iota(jnp.int32, (LANES, half), 1)
                    kt = lax.shift_right_logical(ki, shift)
                    ok = ((qi & (SUB - 1)) == (ki & (SUB - 1))) & (kt <= lax.shift_right_logical(qi, shift)) & (kt < limit)
                    cap[r:r + LANES, :] = jnp.where(ok, OPEN, MASKED)

            for m in range(2):
                xb[(s + 1) % 2, m] = rb[c // chunks, c % chunks * 2 + m].reshape(pairs, per_dev, width)

        after = (s + 1) % (2 * steps) // steps
        norm_next(after, s + 1, 0)
        out(1)
        project_first(0)
        norm()
        up()
        norm_next(after, s + 1, 1)
        project_first(1)
        down(1)
        deliver(1)

        @pl.when(s == steps - 1)
        def _():
            for t in rest:
                load_tile(t, 1).wait()
            for i in range(3):
                load(i, 1).start()

        @pl.when(s == steps - 2)
        def _():
            for t in first:
                load_tile(t, 1).start()

        @pl.when(s + 2 < steps)
        def _():
            for m in range(2):
                load_x(s + 2, m).start()

    for slot in range(steps):
        wait_sent(slot)
    got = y_ref.at[:, :, pl.ds(0, peers * per_dev), :]
    pltpu.make_async_copy(got, got, y_sem).wait()


def solution(mesh):
    act_spec = P('data', 'sp', None, None)
    n_sp = mesh.shape['sp']

    def local_step(latents, valid_len, norm_w, w_qkv, w_out, w_up, w_down):
        videos, frames, rows, width = latents.shape
        heads, head_dim = w_out.shape[1:3]
        hidden = w_up.shape[2]
        tokens = videos * frames * rows
        half = rows // 2
        any_spec = pl.BlockSpec(memory_space=pl.ANY)
        dma = pltpu.SemaphoreType.DMA
        steps = videos * frames
        firsts = len(column_tiles(head_windows(heads, head_dim), 0, (0, 1, 2), width))
        rests = pl.cdiv(3 * width, TILE) - firsts
        return pl.pallas_call(
            functools.partial(kernel, n_sp, heads, head_dim),
            out_shape=pltpu.VMEM(latents.shape, bf16),
            in_specs=[any_spec, pl.BlockSpec(memory_space=pltpu.SMEM), pl.BlockSpec(memory_space=pltpu.VMEM)] + [any_spec] * 4,
            out_specs=pl.BlockSpec(memory_space=pltpu.VMEM),
            scratch_shapes=[
                pltpu.VMEM((rests, width, TILE), bf16), pltpu.VMEM((firsts, width, TILE), bf16),
                pltpu.VMEM((width, width), bf16),
                pltpu.VMEM((width, hidden), bf16), pltpu.VMEM((hidden, width), bf16),
                pltpu.VMEM((2, 2, n_sp // 2, rows // n_sp, width), bf16), pltpu.VMEM((2, half, 2 * width), bf16),
                pltpu.VMEM((width, rows), bf16),
                pltpu.VMEM((half, width), bf16), pltpu.VMEM((half, width), bf16),
                pltpu.VMEM((2, half, width), bf16),
                pltpu.VMEM((half, hidden), bf16), pltpu.VMEM((steps, rows // SUB, SUB, width), bf16),
                pltpu.VMEM((videos, rows // n_sp // SUB, n_sp * frames * SUB, width), bf16), pltpu.VMEM((half, half), f32),
                dma((3,)), dma((rests,)), dma((firsts,)), dma((2, 2)), dma((steps,)), dma((videos,)), dma,
            ],
            compiler_params=pltpu.CompilerParams(collective_id=0, has_side_effects=True, vmem_limit_bytes=62_000_000),
            cost_estimate=pl.CostEstimate(
                flops=2 * 2 * tokens * width * (4 * width + 2 * hidden), bytes_accessed=70_000_000, transcendentals=0),
            name="dit",
        )(latents.reshape(videos, frames, n_sp // 2, 2, rows // n_sp, width), valid_len, norm_w, w_qkv, w_out.reshape(2, width, width), w_up, w_down)

    return jax.shard_map(local_step, mesh=mesh, in_specs=(act_spec, P('data'), P(), P(), P(), P(), P()), out_specs=act_spec, check_vma=False)
```

time: 246 us -> 245 us (level)
  Pallas kernels: 244 us -> 241 us
where the time goes in v5:
time: 245 us; the launch traced here: 244 us
  Pallas kernels  241 us (98%)
    pallas_call x1, Pallas kernels, local_step(): pl.pallas_call(functools.partial(kernel, n_sp, heads, head_dim), out_shap...  241 us

profile of v5, /device:TPU:21, one launch (start us, length us, event | category | flops | bytes accessed | tf_op | source)
XLA Modules:
  0.0 243.7 jit_solution(6665825547416335536)
XLA Ops:
  0.0 241.5 %dit.1 = bf16[2,2,512,1152]{3,2,1,0:T(8,128)(2,1)S(1)} custom-call(bf16[2,2,8,2,32,1152]{5,4,3,2,1,0:T(8,128)(2,1)} %bitcast.3, s32[2]{0:T(128)} %len_ref.1, bf16[2,4,1152]{2,1,0:T(4,128)(2,1)} %norm_ref.1, bf16[2,1152,3456]{2,1,0:T(8,128)(2,1)} %wqkv_hbm.1, bf16[2,1152,1152]{2,1,0:T(8,128)(2,1)} %bitcast.2, bf16[2,1152,4608]{2,1,0:T(8,128)(2,1)} %wup_hbm.1, ...), custom_call_target="tpu_custom_call" | custom-call | flops 130459631616 | bytes 70000000 | tf_op jit(solution)/shard_map/dit/pallas_call | solution.py:394
  241.5 2.2 copy.9

commit v6 on v5

--- a/solution.py
+++ b/solution.py
@@ -209,6 +209,10 @@
             dst_ref=y_ref.at[c // chunks, :, result_rows(c, m), :],
             send_sem=send_sem.at[c], recv_sem=y_sem, device_id={"sp": j}, device_id_type=MESH)
 
+    def pair_at(i):
+        turn = (i + 1) // 2 * (1 - 2 * (i % 2))
+        return lax.rem(me // 2 + pairs // 2 + turn + pairs, pairs)
+
     def wait_sent(slot):
         sent = zb.at[slot, pl.ds(0, peers * groups)]
         pltpu.make_async_copy(sent, sent, send_sem.at[slot]).wait()
@@ -251,8 +255,8 @@
             @pl.when(spatial)
             def _():
                 @pl.loop(0, pairs)
-                def _(k):
-                    pair = lax.rem(me // 2 + k, pairs)
+                def _(i):
+                    pair = pair_at(i)
 
                     @pl.when(2 * pair + m != me)
                     def _():
@@ -265,9 +269,11 @@
 
             @pl.when(temporal)
             def _():
-                @pl.loop(1, n_sp)
-                def _(k):
-                    give(slot, m, lax.rem(me + k, n_sp)).start()
+                @pl.loop(0, pairs - 1)
+                def _(i):
+                    for core in range(2):
+                        give(slot, m, 2 * pair_at(i) + core).start()
+                give(slot, m, me + 1 - 2 * (me % 2)).start()
                 for f in range(frames):
                     y_ref[slot // chunks, f, result_rows(slot, m), :] = zb[slot, (m * n_sp + me) * frames + f]
 
@@ -279,10 +285,12 @@
         def _():
             attention(0, (0,), there, 3, 3, cap)
 
+        for i in range(2):
+            load(i, layer).wait()
+
         @pl.when(slot == 0)
         def _():
-            for i in range(3):
-                load(i, layer).wait()
+            load(2, layer).wait()
 
         @pl.when(temporal)
         def _():
@@ -342,12 +350,14 @@
             for m in range(2):
                 xb[(s + 1) % 2, m] = rb[c // chunks, c % chunks * 2 + m].reshape(pairs, per_dev, width)
 
-        after = (s + 1) % (2 * steps) // steps
+        after = jnp.minimum((s + 1) // steps, 1)
         norm_next(after, s + 1, 0)
         out(1)
+        load(0, after).start()
         project_first(0)
         norm()
         up()
+        load(1, after).start()
         norm_next(after, s + 1, 1)
         project_first(1)
         down(1)
@@ -357,8 +367,7 @@
         def _():
             for t in rest:
                 load_tile(t, 1).wait()
-            for i in range(3):
-                load(i, 1).start()
+            load(2, 1).start()
 
         @pl.when(s == steps - 2)
         def _():
@@ -370,6 +379,8 @@
             for m in range(2):
                 load_x(s + 2, m).start()
 
+    for i in range(2):
+        load(i, 1).wait()
     for slot in range(steps):
         wait_sent(slot)
     got = y_ref.at[:, :, pl.ds(0, peers * per_dev), :]

time: 245 us -> 240 us (0.980)
  Pallas kernels: 241 us -> 236 us
    pallas_call x1, Pallas kernels: 241 us -> 236 us  [local_step(): pl.pallas_call(functools.partial(kernel, n_sp, heads, head_dim), out_shap...]
where the time goes in v6:
time: 240 us; the launch traced here: 238 us
  Pallas kernels  236 us (98%)
    pallas_call x1, Pallas kernels, local_step(): pl.pallas_call(functools.partial(kernel, n_sp, heads, head_dim), out_shap...  236 us

profile of v6, /device:TPU:21, one launch (start us, length us, event | category | flops | bytes accessed | tf_op | source)
XLA Modules:
  0.0 238.4 jit_solution(284689163508719911)
XLA Ops:
  0.0 236.2 %dit.1 = bf16[2,2,512,1152]{3,2,1,0:T(8,128)(2,1)S(1)} custom-call(bf16[2,2,8,2,32,1152]{5,4,3,2,1,0:T(8,128)(2,1)} %bitcast.3, s32[2]{0:T(128)} %len_ref.1, bf16[2,4,1152]{2,1,0:T(4,128)(2,1)} %norm_ref.1, bf16[2,1152,3456]{2,1,0:T(8,128)(2,1)} %wqkv_hbm.1, bf16[2,1152,1152]{2,1,0:T(8,128)(2,1)} %bitcast.2, bf16[2,1152,4608]{2,1,0:T(8,128)(2,1)} %wup_hbm.1, ...), custom_call_target="tpu_custom_call" | custom-call | flops 130459631616 | bytes 70000000 | tf_op jit(solution)/shard_map/dit/pallas_call | solution.py:405
  236.3 2.2 copy.9

commit v7 on v6

--- a/solution.py
+++ b/solution.py
@@ -185,10 +185,6 @@
         load_x(0, m).start()
     for t in first + rest:
         load_tile(t, 0).start()
-    for i in range(3):
-        load(i, 0).start()
-    for m in range(2):
-        load_x(1, m).start()
 
     def frame_rows(s):
         return pl.ds(pl.multiple_of((me * frames + s % frames) * SUB, SUB), SUB)
@@ -221,6 +217,10 @@
         load_x(0, m).wait()
     for t in first:
         load_tile(t, 0).wait()
+    for i in range(3):
+        load(i, 0).start()
+    for m in range(2):
+        load_x(1, m).start()
     for m in range(2):
         norm_next(0, 0, m)
         project_first(m)

time: 240 us -> 237 us (0.988)
  no operation moved by 1% of the time
where the time goes in v7:
time: 237 us
  Pallas kernels  235 us (99%)
    pallas_call x1, Pallas kernels, local_step(): pl.pallas_call(functools.partial(kernel, n_sp, heads, head_dim), out_shap...  235 us

profile of v7, /device:TPU:21, one launch (start us, length us, event | category | flops | bytes accessed | tf_op | source)
XLA Modules:
  0.0 236.7 jit_solution(11033925930597950898)
XLA Ops:
  0.0 234.5 %dit.1 = bf16[2,2,512,1152]{3,2,1,0:T(8,128)(2,1)S(1)} custom-call(bf16[2,2,8,2,32,1152]{5,4,3,2,1,0:T(8,128)(2,1)} %bitcast.3, s32[2]{0:T(128)} %len_ref.1, bf16[2,4,1152]{2,1,0:T(4,128)(2,1)} %norm_ref.1, bf16[2,1152,3456]{2,1,0:T(8,128)(2,1)} %wqkv_hbm.1, bf16[2,1152,1152]{2,1,0:T(8,128)(2,1)} %bitcast.2, bf16[2,1152,4608]{2,1,0:T(8,128)(2,1)} %wup_hbm.1, ...), custom_call_target="tpu_custom_call" | custom-call | flops 130459631616 | bytes 70000000 | tf_op jit(solution)/shard_map/dit/pallas_call | solution.py:405
  234.5 2.2 copy.9

commit v8 on v7

--- a/solution.py
+++ b/solution.py
@@ -205,9 +205,8 @@
             dst_ref=y_ref.at[c // chunks, :, result_rows(c, m), :],
             send_sem=send_sem.at[c], recv_sem=y_sem, device_id={"sp": j}, device_id_type=MESH)
 
-    def pair_at(i):
-        turn = (i + 1) // 2 * (1 - 2 * (i % 2))
-        return lax.rem(me // 2 + pairs // 2 + turn + pairs, pairs)
+    mine = me // 2
+    turns = [(pairs // 2 + (i + 1) // 2 * (1 - 2 * (i % 2))) % pairs for i in range(pairs - 1)]
 
     def wait_sent(slot):
         sent = zb.at[slot, pl.ds(0, peers * groups)]
@@ -251,31 +250,27 @@
             z = residual(hb[...], project(ub[...], wdown[...]))
             zb[slot, m * (half // SUB):(m + 1) * (half // SUB)] = z.reshape(half // SUB, SUB, width)
 
-        def deliver(m):
-            @pl.when(spatial)
+        def keep_frame(m):
+            @pl.when(m == me % 2)
             def _():
-                @pl.loop(0, pairs)
-                def _(i):
-                    pair = pair_at(i)
-
-                    @pl.when(2 * pair + m != me)
-                    def _():
-                        send(s, m, pair).start()
-
-                @pl.when(m == me % 2)
-                def _():
-                    for g in range(groups):
-                        rb[s // frames, g, frame_rows(s), :] = zb[s, (m * pairs + me // 2) * groups + g]
-
-            @pl.when(temporal)
+                for g in range(groups):
+                    rb[s // frames, g, frame_rows(s), :] = zb[s, (m * pairs + mine) * groups + g]
+
+            @pl.when(m != me % 2)
             def _():
-                @pl.loop(0, pairs - 1)
-                def _(i):
-                    for core in range(2):
-                        give(slot, m, 2 * pair_at(i) + core).start()
-                give(slot, m, me + 1 - 2 * (me % 2)).start()
-                for f in range(frames):
-                    y_ref[slot // chunks, f, result_rows(slot, m), :] = zb[slot, (m * n_sp + me) * frames + f]
+                send(s, m, mine).start()
+
+        def send_frame(m):
+            for t in turns:
+                send(s, m, lax.rem(mine + t, pairs)).start()
+
+        def send_result(m):
+            for t in turns:
+                for core in range(2):
+                    give(slot, m, 2 * lax.rem(mine + t, pairs) + core).start()
+            give(slot, m, me + 1 - 2 * (me % 2)).start()
+            for f in range(frames):
+                y_ref[slot // chunks, f, result_rows(slot, m), :] = zb[slot, (m * n_sp + me) * frames + f]
 
         @pl.when(spatial)
         def _():
@@ -307,14 +302,15 @@
         def _():
             pl.semaphore_wait(barrier, peers)
 
-        deliver(0)
-
         @pl.when(spatial)
         def _():
+            keep_frame(0)
+            send_frame(0)
             attention(1, (0, 1), {(t, r) for t in range(tiles) for r in range(2)}, 5, 3, None)
 
         @pl.when(temporal)
         def _():
+            send_result(0)
             attention(1, (1,), there | {(t, 1) for t in extra}, 4, 3, cap)
 
         @pl.when(s == steps - 1)
@@ -361,7 +357,15 @@
         norm_next(after, s + 1, 1)
         project_first(1)
         down(1)
-        deliver(1)
+
+        @pl.when(spatial)
+        def _():
+            keep_frame(1)
+            send_frame(1)
+
+        @pl.when(temporal)
+        def _():
+            send_result(1)
 
         @pl.when(s == steps - 1)
         def _():

time: 237 us -> 238 us (level)
  no operation moved by 1% of the time
where the time goes in v8:
time: 238 us
  Pallas kernels  236 us (99%)
    pallas_call x1, Pallas kernels, local_step(): pl.pallas_call(functools.partial(kernel, n_sp, heads, head_dim), out_shap...  236 us

profile of v8, /device:TPU:21, one launch (start us, length us, event | category | flops | bytes accessed | tf_op | source)
XLA Modules:
  0.0 237.9 jit_solution(16653953298908096804)
XLA Ops:
  0.0 235.7 %dit.1 = bf16[2,2,512,1152]{3,2,1,0:T(8,128)(2,1)S(1)} custom-call(bf16[2,2,8,2,32,1152]{5,4,3,2,1,0:T(8,128)(2,1)} %bitcast.3, s32[2]{0:T(128)} %len_ref.1, bf16[2,4,1152]{2,1,0:T(4,128)(2,1)} %norm_ref.1, bf16[2,1152,3456]{2,1,0:T(8,128)(2,1)} %wqkv_hbm.1, bf16[2,1152,1152]{2,1,0:T(8,128)(2,1)} %bitcast.2, bf16[2,1152,4608]{2,1,0:T(8,128)(2,1)} %wup_hbm.1, ...), custom_call_target="tpu_custom_call" | custom-call | flops 130459631616 | bytes 70000000 | tf_op jit(solution)/shard_map/dit/pallas_call | solution.py:409
  235.7 2.2 copy.9

commit v9 on v7

--- a/solution.py
+++ b/solution.py
@@ -61,12 +61,11 @@
     return slice(t * TILE, min((t + 1) * TILE, 3 * width))
 
 
-def attend(nb, w_of, qk, vt, a_ref, heads, head_dim, mine, key_halves, made, look, lead, cap_ref):
+def attend(nb, w_of, qk, vt, a_ref, heads, head_dim, place, mine, key_halves, made, look, lead, cap_ref):
     _, half, width = nb.shape
     scale = head_dim ** -0.5 * math.log2(math.e)
     wins = head_windows(heads, head_dim)
     made = set(made)
-    key_rows = slice(key_halves[0] * half, (key_halves[-1] + 1) * half)
 
     def pieces(h, parts):
         return [(t, r) for p in parts for t in column_tiles(wins, h, (p,), width) for r in ((mine,) if p == 0 else key_halves)]
@@ -74,10 +73,10 @@
     def make(t, r):
         if (t, r) not in made:
             made.add((t, r))
-            project_piece(nb, w_of(t), qk, vt, t, r)
+            project_piece(nb, w_of(t), qk, vt, t, place(r))
 
     def keys(cols):
-        return jnp.concatenate([qk[r, :, cols] for r in key_halves], axis=0)
+        return jnp.concatenate([qk[place(r), :, cols] for r in key_halves], axis=0)
 
     def scores(h):
         for u in pieces(h, (0, 1)):
@@ -85,7 +84,7 @@
         lo, base, w_ = wins[h]
         lane = lax.broadcasted_iota(jnp.int32, (1, w_), 1) + base
         own = jnp.where((lane >= lo) & (lane < lo + head_dim), 1.0, 0.0).astype(bf16)
-        q = qk[mine, :, base:base + w_] * own
+        q = qk[place(mine), :, base:base + w_] * own
         k = keys(slice(width + base, width + base + w_))
         return lax.dot_general(k, q, (((1,), (1,)), ((), ())), preferred_element_type=f32)
 
@@ -108,7 +107,8 @@
         p = (e * (1.0 / jnp.sum(e, 0, keepdims=True))).astype(bf16)
         lo = h * head_dim
         r0, r1 = lo // PACK * PACK, pl.cdiv(lo + head_dim, PACK) * PACK
-        o = jnp.dot(vt[r0:r1, key_rows], p, preferred_element_type=f32)
+        v = jnp.concatenate([vt[place(r), r0:r1, :] for r in key_halves], axis=1)
+        o = jnp.dot(v, p, preferred_element_type=f32)
         parts.append((lo, o[lo - r0:lo - r0 + head_dim, :]))
         while (done + 1) * LANES <= lo + head_dim:
             g0, g1 = done * LANES, (done + 1) * LANES
@@ -125,7 +125,7 @@
     if cols.start < 2 * width:
         qk[r, :, cols] = piece
     else:
-        vt[cols.start - 2 * width:cols.stop - 2 * width, r * half:(r + 1) * half] = piece.T
+        vt[r, cols.start - 2 * width:cols.stop - 2 * width, :] = piece.T
 
 
 def kernel(n_sp, heads, head_dim, x_hbm, len_ref, norm_ref, wqkv_hbm, wout_hbm, wup_hbm, wdown_hbm, y_ref,
@@ -227,8 +227,9 @@
     for t in rest:
         load_tile(t, 0).wait()
 
-    @pl.loop(0, 2 * steps)
-    def _(s):
+    @pl.loop(0, 4 * steps)
+    def _(turn):
+        s, m = turn // 2, turn % 2
         spatial = s < steps
         temporal = s >= steps
         layer = s // steps
@@ -251,133 +252,135 @@
             z = residual(hb[...], project(ub[...], wdown[...]))
             zb[slot, m * (half // SUB):(m + 1) * (half // SUB)] = z.reshape(half // SUB, SUB, width)
 
-        def deliver(m):
-            @pl.when(spatial)
-            def _():
-                @pl.loop(0, pairs)
-                def _(i):
-                    pair = pair_at(i)
-
-                    @pl.when(2 * pair + m != me)
-                    def _():
-                        send(s, m, pair).start()
-
-                @pl.when(m == me % 2)
+        def second():
+            @pl.when(s == steps - 1)
+            def _():
+                for t in rest:
+                    load_tile(t, 1).start()
+                for t in first:
+                    load_tile(t, 1).wait()
+
+            @pl.when(s + 1 < steps)
+            def _():
+                for m in range(2):
+                    load_x(s + 1, m).wait()
+
+            @pl.when(jnp.logical_and(s + 1 >= steps, s + 1 < 2 * steps))
+            def _():
+                c = s + 1 - steps
+
+                @pl.when(c % chunks == 0)
                 def _():
-                    for g in range(groups):
-                        rb[s // frames, g, frame_rows(s), :] = zb[s, (m * pairs + me // 2) * groups + g]
+                    v = c // chunks
+                    got = rb.at[v, :, pl.ds(0, peers * frames * SUB), :]
+                    pltpu.make_async_copy(got, got, recv_sem.at[v]).wait()
+                    shift = SUB.bit_length() - 1
+                    limit = len_ref[v]
+                    for r in range(0, half, LANES):
+                        ki = lax.broadcasted_iota(jnp.int32, (LANES, half), 0) + r
+                        qi = lax.broadcasted_iota(jnp.int32, (LANES, half), 1)
+                        kt = lax.shift_right_logical(ki, shift)
+                        ok = ((qi & (SUB - 1)) == (ki & (SUB - 1))) & (kt <= lax.shift_right_logical(qi, shift)) & (kt < limit)
+                        cap[r:r + LANES, :] = jnp.where(ok, OPEN, MASKED)
+
+                for m in range(2):
+                    xb[(s + 1) % 2, m] = rb[c // chunks, c % chunks * 2 + m].reshape(pairs, per_dev, width)
+
+            after = jnp.minimum((s + 1) // steps, 1)
+            norm_next(after, s + 1, 0)
+            out(1)
+            load(0, after).start()
+            project_first(0)
+            norm()
+            up()
+            load(1, after).start()
+            norm_next(after, s + 1, 1)
+            project_first(1)
+            down(1)
+
+        @pl.when(jnp.logical_and(spatial, m == 0))
+        def _():
+            attention(lambda r: r, 0, (0, 1), there, 3, 2, None)
+
+        @pl.when(jnp.logical_and(spatial, m == 1))
+        def _():
+            attention(lambda r: r, 1, (0, 1), {(t, r) for t in range(tiles) for r in range(2)}, 5, 3, None)
+
+        @pl.when(temporal)
+        def _():
+            attention(lambda r: m, 0, (0,), there, 3, 3, cap)
+
+        @pl.when(m == 0)
+        def _():
+            for i in range(2):
+                load(i, layer).wait()
+
+            @pl.when(slot == 0)
+            def _():
+                load(2, layer).wait()
 
             @pl.when(temporal)
             def _():
-                @pl.loop(0, pairs - 1)
-                def _(i):
-                    for core in range(2):
-                        give(slot, m, 2 * pair_at(i) + core).start()
-                give(slot, m, me + 1 - 2 * (me % 2)).start()
-                for f in range(frames):
-                    y_ref[slot // chunks, f, result_rows(slot, m), :] = zb[slot, (m * n_sp + me) * frames + f]
+                wait_sent(slot)
+
+            out(0)
+            for t in extra:
+                project_piece(n1, w_of(t), qk, vt, t, 1)
+            norm()
+            up()
+            down(0)
+
+            @pl.when(s == 0)
+            def _():
+                pl.semaphore_wait(barrier, peers)
+
+        @pl.when(m == 1)
+        def _():
+            second()
 
         @pl.when(spatial)
         def _():
-            attention(0, (0, 1), there, 3, 2, None)
+            @pl.loop(0, pairs)
+            def _(i):
+                pair = pair_at(i)
+
+                @pl.when(2 * pair + m != me)
+                def _():
+                    send(s, m, pair).start()
+
+            @pl.when(m == me % 2)
+            def _():
+                for g in range(groups):
+                    rb[s // frames, g, frame_rows(s), :] = zb[s, (m * pairs + me // 2) * groups + g]
 
         @pl.when(temporal)
         def _():
-            attention(0, (0,), there, 3, 3, cap)
-
-        for i in range(2):
-            load(i, layer).wait()
-
-        @pl.when(slot == 0)
-        def _():
-            load(2, layer).wait()
-
-        @pl.when(temporal)
-        def _():
-            wait_sent(slot)
-
-        out(0)
-        for t in extra:
-            project_piece(n1, w_of(t), qk, vt, t, 1)
-        norm()
-        up()
-        down(0)
-
-        @pl.when(s == 0)
-        def _():
-            pl.semaphore_wait(barrier, peers)
-
-        deliver(0)
-
-        @pl.when(spatial)
-        def _():
-            attention(1, (0, 1), {(t, r) for t in range(tiles) for r in range(2)}, 5, 3, None)
-
-        @pl.when(temporal)
-        def _():
-            attention(1, (1,), there | {(t, 1) for t in extra}, 4, 3, cap)
-
-        @pl.when(s == steps - 1)
-        def _():
-            for t in rest:
-                load_tile(t, 1).start()
-            for t in first:
-                load_tile(t, 1).wait()
-
-        @pl.when(s + 1 < steps)
-        def _():
-            for m in range(2):
-                load_x(s + 1, m).wait()
-
-        @pl.when(jnp.logical_and(s + 1 >= steps, s + 1 < 2 * steps))
-        def _():
-            c = s + 1 - steps
-
-            @pl.when(c % chunks == 0)
-            def _():
-                v = c // chunks
-                got = rb.at[v, :, pl.ds(0, peers * frames * SUB), :]
-                pltpu.make_async_copy(got, got, recv_sem.at[v]).wait()
-                shift = SUB.bit_length() - 1
-                limit = len_ref[v]
-                for r in range(0, half, LANES):
-                    ki = lax.broadcasted_iota(jnp.int32, (LANES, half), 0) + r
-                    qi = lax.broadcasted_iota(jnp.int32, (LANES, half), 1)
-                    kt = lax.shift_right_logical(ki, shift)
-                    ok = ((qi & (SUB - 1)) == (ki & (SUB - 1))) & (kt <= lax.shift_right_logical(qi, shift)) & (kt < limit)
-                    cap[r:r + LANES, :] = jnp.where(ok, OPEN, MASKED)
-
-            for m in range(2):
-                xb[(s + 1) % 2, m] = rb[c // chunks, c % chunks * 2 + m].reshape(pairs, per_dev, width)
-
-        after = jnp.minimum((s + 1) // steps, 1)
-        norm_next(after, s + 1, 0)
-        out(1)
-        load(0, after).start()
-        project_first(0)
-        norm()
-        up()
-        load(1, after).start()
-        norm_next(after, s + 1, 1)
-        project_first(1)
-        down(1)
-        deliver(1)
-
-        @pl.when(s == steps - 1)
-        def _():
-            for t in rest:
-                load_tile(t, 1).wait()
-            load(2, 1).start()
-
-        @pl.when(s == steps - 2)
-        def _():
-            for t in first:
-                load_tile(t, 1).start()
-
-        @pl.when(s + 2 < steps)
-        def _():
-            for m in range(2):
-                load_x(s + 2, m).start()
+            @pl.loop(0, pairs - 1)
+            def _(i):
+                for core in range(2):
+                    give(slot, m, 2 * pair_at(i) + core).start()
+            give(slot, m, me + 1 - 2 * (me % 2)).start()
+            for f in range(frames):
+                y_ref[slot // chunks, f, result_rows(slot, m), :] = zb[slot, (m * n_sp + me) * frames + f]
+
+        @pl.when(m == 1)
+        def _():
+
+            @pl.when(s == steps - 1)
+            def _():
+                for t in rest:
+                    load_tile(t, 1).wait()
+                load(2, 1).start()
+
+            @pl.when(s == steps - 2)
+            def _():
+                for t in first:
+                    load_tile(t, 1).start()
+
+            @pl.when(s + 2 < steps)
+            def _():
+                for m in range(2):
+                    load_x(s + 2, m).start()
 
     for i in range(2):
         load(i, 1).wait()
@@ -412,7 +415,7 @@
                 pltpu.VMEM((width, width), bf16),
                 pltpu.VMEM((width, hidden), bf16), pltpu.VMEM((hidden, width), bf16),
                 pltpu.VMEM((2, 2, n_sp // 2, rows // n_sp, width), bf16), pltpu.VMEM((2, half, 2 * width), bf16),
-                pltpu.VMEM((width, rows), bf16),
+                pltpu.VMEM((2, width, half), bf16),
                 pltpu.VMEM((half, width), bf16), pltpu.VMEM((half, width), bf16),
                 pltpu.VMEM((2, half, width), bf16),
                 pltpu.VMEM((half, hidden), bf16), pltpu.VMEM((steps, rows // SUB, SUB, width), bf16),

time: 237 us -> 240 us (1.013); the launches traced: 237 us -> 237 us
  no operation moved by 1% of the time
where the time goes in v9:
time: 240 us; the launch traced here: 237 us
  Pallas kernels  235 us (98%)
    pallas_call x1, Pallas kernels, local_step(): pl.pallas_call(functools.partial(kernel, n_sp, heads, head_dim), out_shap...  235 us

profile of v9, /device:TPU:21, one launch (start us, length us, event | category | flops | bytes accessed | tf_op | source)
XLA Modules:
  0.0 236.7 jit_solution(1322591367039975048)
XLA Ops:
  0.0 234.5 %dit.1 = bf16[2,2,512,1152]{3,2,1,0:T(8,128)(2,1)S(1)} custom-call(bf16[2,2,8,2,32,1152]{5,4,3,2,1,0:T(8,128)(2,1)} %bitcast.3, s32[2]{0:T(128)} %len_ref.1, bf16[2,4,1152]{2,1,0:T(4,128)(2,1)} %norm_ref.1, bf16[2,1152,3456]{2,1,0:T(8,128)(2,1)} %wqkv_hbm.1, bf16[2,1152,1152]{2,1,0:T(8,128)(2,1)} %bitcast.2, bf16[2,1152,4608]{2,1,0:T(8,128)(2,1)} %wup_hbm.1, ...), custom_call_target="tpu_custom_call" | custom-call | flops 130459631616 | bytes 70000000 | tf_op jit(solution)/shard_map/dit/pallas_call | solution.py:408
  234.5 2.2 copy.9

commit v10 on v7

--- a/solution.py
+++ b/solution.py
@@ -14,6 +14,7 @@
 LANES = 128
 TILE = 256
 SUB = 8
+FILL = 4
 PACK = 16
 f32, bf16 = jnp.float32, jnp.bfloat16
 MESH = pl.DeviceIdType.MESH
@@ -61,7 +62,7 @@
     return slice(t * TILE, min((t + 1) * TILE, 3 * width))
 
 
-def attend(nb, w_of, qk, vt, a_ref, heads, head_dim, mine, key_halves, made, look, lead, cap_ref):
+def attend(nb, w_of, qk, vt, a_ref, heads, head_dim, mine, key_halves, made, look, lead, cap_ref, fill=()):
     _, half, width = nb.shape
     scale = head_dim ** -0.5 * math.log2(math.e)
     wins = head_windows(heads, head_dim)
@@ -106,6 +107,10 @@
             s = jnp.minimum(s, cap_ref[...])
         e = jnp.exp2((s - jnp.max(s, 0, keepdims=True)) * scale)
         p = (e * (1.0 / jnp.sum(e, 0, keepdims=True))).astype(bf16)
+        if h >= heads - FILL:
+            for f in fill[:pl.cdiv(len(fill), heads - h)]:
+                f()
+                fill = fill[1:]
         lo = h * head_dim
         r0, r1 = lo // PACK * PACK, pl.cdiv(lo + head_dim, PACK) * PACK
         o = jnp.dot(vt[r0:r1, key_rows], p, preferred_element_type=f32)
@@ -129,7 +134,7 @@
 
 
 def kernel(n_sp, heads, head_dim, x_hbm, len_ref, norm_ref, wqkv_hbm, wout_hbm, wup_hbm, wdown_hbm, y_ref,
-           wrest, wfirst, wout, wup, wdown, xb, qk, vt, ab, hb, n1, ub, zb, rb, cap,
+           wrest, wfirst, wout, wup, wdown, xb, qk, vt, ab, hb, n1, acc, ub, zb, rb, cap,
            w_sem, rest_sem, first_sem, x_sem, send_sem, recv_sem, y_sem):
     videos, frames, pairs, _, per_dev, width = x_hbm.shape
     rows = pairs * 2 * per_dev
@@ -185,6 +190,7 @@
         load_x(0, m).start()
     for t in first + rest:
         load_tile(t, 0).start()
+    load(0, 0).start()
 
     def frame_rows(s):
         return pl.ds(pl.multiple_of((me * frames + s % frames) * SUB, SUB), SUB)
@@ -217,7 +223,7 @@
         load_x(0, m).wait()
     for t in first:
         load_tile(t, 0).wait()
-    for i in range(3):
+    for i in range(1, 3):
         load(i, 0).start()
     for m in range(2):
         load_x(1, m).start()
@@ -240,6 +246,18 @@
         def out(m):
             hb[...] = residual(xs[m].reshape(half, width), project(ab[...], wout[...]))
 
+        depth = width * 2 // 3 // TILE * TILE
+
+        def out_start(j):
+            cols = slice(j, min(j + TILE, width))
+            acc[:, cols] = jnp.dot(ab[:, :depth], wout[:depth, cols], preferred_element_type=f32)
+
+        def out_rest(m):
+            late = jnp.dot(ab[:, depth:], wout[depth:, :], preferred_element_type=f32)
+            hb[...] = residual(xs[m].reshape(half, width), (acc[...] + late).astype(bf16))
+
+        early = [functools.partial(out_start, j) for j in range(0, width, TILE)]
+
         def norm():
             norms = norm_ref[layer].astype(f32)
             ab[...] = layer_norm(hb[...], norms[2:3], norms[3:4])
@@ -254,13 +272,12 @@
         def deliver(m):
             @pl.when(spatial)
             def _():
-                @pl.loop(0, pairs)
-                def _(i):
-                    pair = pair_at(i)
-
-                    @pl.when(2 * pair + m != me)
-                    def _():
-                        send(s, m, pair).start()
+                for i in range(pairs - 1):
+                    send(s, m, pair_at(i)).start()
+
+                @pl.when(m != me % 2)
+                def _():
+                    send(s, m, me // 2).start()
 
                 @pl.when(m == me % 2)
                 def _():
@@ -277,16 +294,17 @@
                 for f in range(frames):
                     y_ref[slot // chunks, f, result_rows(slot, m), :] = zb[slot, (m * n_sp + me) * frames + f]
 
+        load(0, layer).wait()
+
         @pl.when(spatial)
         def _():
-            attention(0, (0, 1), there, 3, 2, None)
+            attention(0, (0, 1), there, 3, 2, None, early)
 
         @pl.when(temporal)
         def _():
-            attention(0, (0,), there, 3, 3, cap)
-
-        for i in range(2):
-            load(i, layer).wait()
+            attention(0, (0,), there, 3, 3, cap, early)
+
+        load(1, layer).wait()
 
         @pl.when(slot == 0)
         def _():
@@ -296,7 +314,7 @@
         def _():
             wait_sent(slot)
 
-        out(0)
+        out_rest(0)
         for t in extra:
             project_piece(n1, w_of(t), qk, vt, t, 1)
         norm()
@@ -415,7 +433,7 @@
                 pltpu.VMEM((width, rows), bf16),
                 pltpu.VMEM((half, width), bf16), pltpu.VMEM((half, width), bf16),
                 pltpu.VMEM((2, half, width), bf16),
-                pltpu.VMEM((half, hidden), bf16), pltpu.VMEM((steps, rows // SUB, SUB, width), bf16),
+                pltpu.VMEM((half, width), f32), pltpu.VMEM((half, hidden), bf16), pltpu.VMEM((steps, rows // SUB, SUB, width), bf16),
                 pltpu.VMEM((videos, rows // n_sp // SUB, n_sp * frames * SUB, width), bf16), pltpu.VMEM((half, half), f32),
                 dma((3,)), dma((rests,)), dma((firsts,)), dma((2, 2)), dma((steps,)), dma((videos,)), dma,
             ],

time: 237 us -> 235 us (level)
  Pallas kernels: 235 us -> 232 us
where the time goes in v10:
time: 235 us; the launch traced here: 234 us
  Pallas kernels  232 us (99%)
    pallas_call x1, Pallas kernels, local_step(): pl.pallas_call(functools.partial(kernel, n_sp, heads, head_dim), out_shap...  232 us

profile of v10, /device:TPU:21, one launch (start us, length us, event | category | flops | bytes accessed | tf_op | source)
XLA Modules:
  0.0 234.4 jit_solution(15209032196602012581)
XLA Ops:
  0.0 232.2 %dit.1 = bf16[2,2,512,1152]{3,2,1,0:T(8,128)(2,1)S(1)} custom-call(bf16[2,2,8,2,32,1152]{5,4,3,2,1,0:T(8,128)(2,1)} %bitcast.3, s32[2]{0:T(128)} %len_ref.1, bf16[2,4,1152]{2,1,0:T(4,128)(2,1)} %norm_ref.1, bf16[2,1152,3456]{2,1,0:T(8,128)(2,1)} %wqkv_hbm.1, bf16[2,1152,1152]{2,1,0:T(8,128)(2,1)} %bitcast.2, bf16[2,1152,4608]{2,1,0:T(8,128)(2,1)} %wup_hbm.1, ...), custom_call_target="tpu_custom_call" | custom-call | flops 130459631616 | bytes 70000000 | tf_op jit(solution)/shard_map/dit/pallas_call | solution.py:423
  232.2 2.2 copy.9

commit v11 on v10

--- a/solution.py
+++ b/solution.py
@@ -10,7 +10,7 @@
 
 LN_EPS = 1e-6
 MASKED = -1e30
-OPEN = 3e38
+OPEN = math.inf
 LANES = 128
 TILE = 256
 SUB = 8
@@ -363,7 +363,7 @@
                     qi = lax.broadcasted_iota(jnp.int32, (LANES, half), 1)
                     kt = lax.shift_right_logical(ki, shift)
                     ok = ((qi & (SUB - 1)) == (ki & (SUB - 1))) & (kt <= lax.shift_right_logical(qi, shift)) & (kt < limit)
-                    cap[r:r + LANES, :] = jnp.where(ok, OPEN, MASKED)
+                    cap[r:r + LANES, :] = jnp.where(ok, OPEN, MASKED * head_dim ** 0.5)
 
             for m in range(2):
                 xb[(s + 1) % 2, m] = rb[c // chunks, c % chunks * 2 + m].reshape(pairs, per_dev, width)

time: 235 us -> 235 us (level)
  no operation moved by 1% of the time
where the time goes in v11:
time: 235 us; the launch traced here: 234 us
  Pallas kernels  232 us (99%)
    pallas_call x1, Pallas kernels, local_step(): pl.pallas_call(functools.partial(kernel, n_sp, heads, head_dim), out_shap...  232 us

profile of v11, /device:TPU:21, one launch (start us, length us, event | category | flops | bytes accessed | tf_op | source)
XLA Modules:
  0.0 234.4 jit_solution(9248865741435116541)
XLA Ops:
  0.0 232.2 %dit.1 = bf16[2,2,512,1152]{3,2,1,0:T(8,128)(2,1)S(1)} custom-call(bf16[2,2,8,2,32,1152]{5,4,3,2,1,0:T(8,128)(2,1)} %bitcast.3, s32[2]{0:T(128)} %len_ref.1, bf16[2,4,1152]{2,1,0:T(4,128)(2,1)} %norm_ref.1, bf16[2,1152,3456]{2,1,0:T(8,128)(2,1)} %wqkv_hbm.1, bf16[2,1152,1152]{2,1,0:T(8,128)(2,1)} %bitcast.2, bf16[2,1152,4608]{2,1,0:T(8,128)(2,1)} %wup_hbm.1, ...), custom_call_target="tpu_custom_call" | custom-call | flops 130459631616 | bytes 70000000 | tf_op jit(solution)/shard_map/dit/pallas_call | solution.py:423
  232.2 2.2 copy.9
